TPU v7x, 512 devices: a whole 4x8x8 slice. The times are simulated.
512 devices in a mesh: batch: 64 (over z, y), tensor: 4 (over x), section: 2 (over core).
Axes of the slice: x: 4, y: 8, z: 8, core: 2. Of those that a mesh axis runs over, the one named last changes fastest.
Arguments:
- prefill_cache: bfloat16 [2, 512, 2, 4, 256, 128], P('section', ('batch', 'tensor')), may hold values from -5 to 5
- lengths: int32 [256], P('batch'), may hold values from 1 to 1280, as said below
- page_table: int32 [256, 5], P('batch'), may hold values from -1 to 7, as said below
- holder: int32 [64, 8], replicated, may hold values from 0 to 63, as said below
- queries: bfloat16 [256, 2, 4, 32, 128], P(('batch', 'section'), None, None, 'tensor'), may hold values from -120 to 120
- new_kv: bfloat16 [256, 2, 4, 2, 4, 128], P(('batch', 'section'), None, None, None, 'tensor'), may hold values from -5 to 5
Outputs:
- attended: bfloat16 [256, 2, 4, 32, 128], P(('batch', 'section'), None, None, 'tensor')
- decode_pool: bfloat16 [2, 512, 2, 4, 256, 128], P('section', 'batch', None, 'tensor')
Inputs may be any that keep to these rules, and one draw needn't show every extreme that they name: Request r's prompt has lengths[r] tokens, held in ceil(lengths[r] / 256) pages. `page_table`: row r names in its first ceil(lengths[r] / 256) columns the pool positions (0 to 7) of the request's pages in order, and -1 after; a position is named at most once among the 4 requests of one batch index; some batch index uses all 8 positions. holder[b, q] = b XOR key_q (bitwise exclusive or of the binary digits), where key_0 to key_7 are distinct numbers of 0 to 63; so each column is a permutation of the batch indices and each row names distinct ones.
All inputs are finite; a program needn't handle non-finite values.
Results may differ from a plain program's by a relative error of at most 0.0038.
Values may be sent and summed in bfloat16 or wider, within the bound.
No kernel may reach another device: no remote copies, remote signals or barrier semaphores. Data moves between devices by JAX's collectives and lax.ppermute only.
A program may use at most 64 MiB of HBM per device.

v0:
```python
import math

import jax
import jax.numpy as jnp
from jax import lax
from jax.sharding import PartitionSpec as P

MASKED = -1e30


def shortened(shard):
    return jax.tree.map(lambda a: a.astype(jnp.bfloat16) if a.dtype == jnp.float32 else a, shard)


def partner_2(value, axis, bit):
    mask = 2**bit
    pairs = [(source, source ^ mask) for source in range(lax.axis_size(axis))]
    return lax.ppermute(value, axis, pairs)


def sent_together(arrays, axis, split_dim, concat_dim, along):
    widths = [math.prod(a.shape[along:]) for a in arrays]
    both = jnp.concatenate(
        [a.reshape(*a.shape[:along], w) for a, w in zip(arrays, widths)], axis=along
    )
    result = lax.all_to_all(both, axis, split_axis=split_dim, concat_axis=concat_dim, tiled=True)
    blocks = jnp.split(result, [sum(widths[:k]) for k in range(1, len(widths))], axis=along)
    return tuple(
        (b.reshape(*result.shape[:along], *a.shape[along:]) for a, b in zip(arrays, blocks))
    )


def page_partials(queries_at, key_rows, value_rows, token_mask):
    score_scale = 1.0 / math.sqrt(key_rows.shape[-1])
    scores = (
        jnp.einsum("nigex,ngpx->ngiep", queries_at, key_rows, preferred_element_type=jnp.float32)
        * score_scale
    )
    page_peak = jnp.max(jnp.where(token_mask, scores, MASKED), axis=-1)
    weights = jnp.where(token_mask, jnp.exp(scores - page_peak[..., None]), 0.0).astype(
        jnp.bfloat16
    )
    weight_sum = jnp.sum(weights.astype(jnp.float32), axis=-1)
    page_output = jnp.einsum(
        "ngiep,ngpx->ngiex", weights, value_rows, preferred_element_type=jnp.float32
    )
    return (page_peak, weight_sum, page_output)


def pick_where(take, partner, current):
    return tuple(
        (
            jnp.where(take.reshape((-1,) + (1,) * (own.ndim - 1)), other, own)
            for other, own in zip(partner, current)
        )
    )


def on_device(prefill_cache, lengths, page_table, holder, queries, new_kv):
    batch_count, positions = holder.shape
    route_keys = holder[0]
    route_bits = lax.axis_size("batch").bit_length() - 1
    local_pages = lax.all_to_all(prefill_cache, "tensor", split_axis=3, concat_axis=1, tiled=True)[
        0
    ]
    kv_local, page_len, head_dim = (
        local_pages.shape[2],
        local_pages.shape[3],
        local_pages.shape[4],
    )
    owned_rows, layers, step_count = (queries.shape[0], queries.shape[1], queries.shape[2])
    group_size = queries.shape[3] // kv_local
    req_count, max_pages = page_table.shape
    layer_rows = lax.all_to_all(queries, "section", split_axis=1, concat_axis=0, tiled=True)
    local_queries = layer_rows[:, 0].reshape(req_count, step_count, kv_local, group_size, head_dim)
    slot_ids = jnp.arange(positions, dtype=jnp.int32)
    page_hits = (page_table[:, :, None] == slot_ids).astype(jnp.int32)
    in_use = jnp.sum(page_hits, axis=(0, 1)) > 0
    request_of = jnp.sum(
        page_hits * jnp.arange(req_count, dtype=jnp.int32)[:, None, None], axis=(0, 1)
    )
    page_of = jnp.sum(
        page_hits * jnp.arange(max_pages, dtype=jnp.int32)[None, :, None], axis=(0, 1)
    )
    length_of = jnp.sum(page_hits * lengths[:, None, None], axis=(0, 1))
    live_count = jnp.clip(length_of - page_of * page_len, 0, page_len)
    position_queries = jnp.take(local_queries, request_of, axis=0)
    send_pages = jnp.where(
        in_use[:, None, None, None, None], local_pages, jnp.zeros((), local_pages.dtype)
    )
    token_index = jnp.arange(page_len, dtype=jnp.int32)
    moving = (send_pages,)
    for bit in range(route_bits):
        take = route_keys // (1 << bit) % 2 == 1
        partner = jax.tree.map(
            lambda part, own: part.astype(own.dtype),
            partner_2(shortened(moving), "batch", bit),
            moving,
        )
        moving = pick_where(take, partner, moving)
    decode_slots = moving[0]
    token_mask = token_index[None, None, None, None, :] < live_count[:, None, None, None, None]
    page_peak, weight_sum, page_output = page_partials(
        position_queries, local_pages[:, 0], local_pages[:, 1], token_mask
    )
    mine = (request_of[None, :] == jnp.arange(req_count, dtype=jnp.int32)[:, None]) & in_use[
        None, :
    ]
    row_mask = mine[:, :, None, None, None]
    request_peak = jnp.max(jnp.where(row_mask, page_peak[None], MASKED), axis=1)
    factor = jnp.where(row_mask, jnp.exp(page_peak[None] - request_peak[:, None]), 0.0)
    numerator = jnp.einsum(
        "rqgie,qgiex->rgiex", factor, page_output, precision=lax.Precision.HIGHEST
    )
    denominator = jnp.sum(factor * weight_sum[None], axis=1)
    numerator, request_peak, denominator = sent_together(
        (numerator[:, None], request_peak[:, None], denominator[:, None]), "section", 0, 1, 5
    )
    flat_queries = queries.reshape(owned_rows * layers, step_count, kv_local, group_size, head_dim)
    new_keys = jnp.transpose(
        new_kv[:, :, :, 0].reshape(owned_rows * layers, step_count, kv_local, head_dim),
        (0, 2, 1, 3),
    )
    new_values = jnp.transpose(
        new_kv[:, :, :, 1].reshape(owned_rows * layers, step_count, kv_local, head_dim),
        (0, 2, 1, 3),
    )
    step_index = jnp.arange(step_count, dtype=jnp.int32)
    causal = step_index[None, :] <= step_index[:, None]
    new_peak, new_sum, new_output = page_partials(
        flat_queries, new_keys, new_values, causal[None, None, :, None, :]
    )
    new_peak = new_peak.reshape(request_peak.shape)
    new_sum = new_sum.reshape(denominator.shape)
    new_output = new_output.reshape(numerator.shape)
    joint_peak = jnp.maximum(request_peak, new_peak)
    old_scale = jnp.exp(request_peak - joint_peak)
    new_scale = jnp.exp(new_peak - joint_peak)
    result = (old_scale[..., None] * numerator + new_scale[..., None] * new_output) / (
        old_scale * denominator + new_scale * new_sum
    )[..., None]
    attended = (
        jnp.transpose(result, (0, 1, 3, 2, 4, 5))
        .reshape(owned_rows, layers, step_count, kv_local * group_size, head_dim)
        .astype(jnp.bfloat16)
    )
    return (attended, decode_slots.reshape((1,) + decode_slots.shape))


def solution(mesh):
    placed = (
        P("section", ("batch", "tensor"), None, None, None, None),
        P("batch"),
        P("batch", None),
        P(),
        P(("batch", "section"), None, None, "tensor", None),
        P(("batch", "section"), None, None, None, "tensor", None),
    )
    return jax.shard_map(
        on_device,
        mesh=mesh,
        in_specs=placed,
        out_specs=(
            P(("batch", "section"), None, None, "tensor", None),
            P("section", "batch", None, "tensor", None, None),
        ),
        check_vma=False,
    )
```

profile of v0, /device:TPU:56, one launch (start us, length us, event | category | flops | bytes accessed | tf_op | source)
XLA Modules:
  0.0 290.6 jit_solution(2103394262275682429)
XLA Ops:
  0.6 2.3 copy.109
  2.9 4.4 %all-to-all-start.1 = ((bf16[1,2,2,4,256,128]{5,4,2,1,0,3:T(8,128)(2,1)}), bf16[1,2,2,4,256,128]{5,4,2,1,0,3:T(8,128)(2,1)S(1)}, u32[]{:S(2)}, u32[]{:S(2)}) async-start(bf16[1,2,2,4,256,128]{5,4,2,1,0,3:T(8,128)(2,1)} %copy.109), calls=%async_computation.1 | async-start | bytes 2097152 | tf_op jit(solution)/shard_map/all_to_all | solution.py:63
  7.5 0.1 convert_reduce_fusion.2
  7.6 14.9 %all-to-all-done.1 = bf16[1,2,2,4,256,128]{5,4,2,1,0,3:T(8,128)(2,1)S(1)} async-done(((bf16[1,2,2,4,256,128]{5,4,2,1,0,3:T(8,128)(2,1)}), bf16[1,2,2,4,256,128]{5,4,2,1,0,3:T(8,128)(2,1)S(1)}, u32[]{:S(2)}, u32[]{:S(2)}) %all-to-all-start.1) | async-done | bytes 1048608 | tf_op jit(solution)/shard_map/all_to_all | solution.py:63
  22.6 0.1 broadcast_select_fusion
  22.7 3.3 %collective-permute-start = (bf16[8,2,1,256,128]{4,3,0,2,1:T(8,128)(2,1)S(1)}, bf16[8,2,1,256,128]{4,3,0,2,1:T(8,128)(2,1)S(1)}, u32[]{:S(2)}, u32[]{:S(2)}) collective-permute-start(bf16[8,2,1,256,128]{4,3,0,2,1:T(8,128)(2,1)S(1)} %broadcast_select_fusion), channel_id=1, source_target_pairs={{0,8},{8,0},{16,24},{24,16},{32,40},{40,32},{48,56},{56,48},{64,72... | collective-permute-start | bytes 3145736 | tf_op jit(solution)/shard_map/ppermute | solution.py:18
  26.0 0.1 slice_reduce_fusion
  26.1 0.6 fusion.21
  26.7 21.7 %collective-permute-done = bf16[8,2,1,256,128]{4,3,0,2,1:T(8,128)(2,1)S(1)} collective-permute-done((bf16[8,2,1,256,128]{4,3,0,2,1:T(8,128)(2,1)S(1)}, bf16[8,2,1,256,128]{4,3,0,2,1:T(8,128)(2,1)S(1)}, u32[]{:S(2)}, u32[]{:S(2)}) %collective-permute-start) | collective-permute-done | bytes 1048608 | tf_op jit(solution)/shard_map/ppermute | solution.py:18
  48.4 0.2 broadcast_select_fusion.1
  48.6 4.0 %collective-permute-start.1 = (bf16[8,2,1,256,128]{4,3,0,2,1:T(8,128)(2,1)S(1)}, bf16[8,2,1,256,128]{4,3,0,2,1:T(8,128)(2,1)S(1)}, u32[]{:S(2)}, u32[]{:S(2)}) collective-permute-start(bf16[8,2,1,256,128]{4,3,0,2,1:T(8,128)(2,1)S(1)} %broadcast_select_fusion.1), channel_id=1, source_target_pairs={{0,16},{8,24},{16,0},{24,8},{32,48},{40,56},{48,32},{56,40},{64,80... | collective-permute-start | bytes 3145736 | tf_op jit(solution)/shard_map/ppermute | solution.py:18
  52.6 44.1 %collective-permute-done.1 = bf16[8,2,1,256,128]{4,3,0,2,1:T(8,128)(2,1)S(1)} collective-permute-done((bf16[8,2,1,256,128]{4,3,0,2,1:T(8,128)(2,1)S(1)}, bf16[8,2,1,256,128]{4,3,0,2,1:T(8,128)(2,1)S(1)}, u32[]{:S(2)}, u32[]{:S(2)}) %collective-permute-start.1) | collective-permute-done | bytes 1048608 | tf_op jit(solution)/shard_map/ppermute | solution.py:18
  96.7 0.2 broadcast_select_fusion.2
  96.9 4.6 %collective-permute-start.2 = (bf16[8,2,1,256,128]{4,3,0,2,1:T(8,128)(2,1)S(1)}, bf16[8,2,1,256,128]{4,3,0,2,1:T(8,128)(2,1)}, u32[]{:S(2)}, u32[]{:S(2)}) collective-permute-start(bf16[8,2,1,256,128]{4,3,0,2,1:T(8,128)(2,1)S(1)} %broadcast_select_fusion.2), channel_id=1, source_target_pairs={{0,32},{8,40},{16,48},{24,56},{32,0},{40,8},{48,16},{56,24},{64,96... | collective-permute-start | bytes 3145736 | tf_op jit(solution)/shard_map/ppermute | solution.py:18
  101.5 0.6 copy.108
  102.1 3.3 %all-to-all-start = ((bf16[2,2,4,8,128]{4,3,2,0,1:T(8,128)(2,1)}), bf16[2,2,4,8,128]{4,3,2,0,1:T(8,128)(2,1)S(1)}, u32[]{:S(2)}, u32[]{:S(2)}) async-start(bf16[2,2,4,8,128]{4,3,2,0,1:T(8,128)(2,1)} %copy.108), calls=%async_computation | async-start | bytes 65536 | tf_op jit(solution)/shard_map/all_to_all | solution.py:74
  105.5 0.3 select_reduce_fusion.2
  105.8 43.8 %collective-permute-done.2 = bf16[8,2,1,256,128]{4,3,0,2,1:T(8,128)(2,1)} collective-permute-done((bf16[8,2,1,256,128]{4,3,0,2,1:T(8,128)(2,1)S(1)}, bf16[8,2,1,256,128]{4,3,0,2,1:T(8,128)(2,1)}, u32[]{:S(2)}, u32[]{:S(2)}) %collective-permute-start.2) | collective-permute-done | bytes 1048608 | tf_op jit(solution)/shard_map/ppermute | solution.py:18
  149.6 1.4 broadcast_select_fusion.3
  151.0 4.3 %collective-permute-start.3 = (bf16[8,2,1,256,128]{4,3,0,2,1:T(8,128)(2,1)S(1)}, bf16[8,2,1,256,128]{4,3,0,2,1:T(8,128)(2,1)}, u32[]{:S(2)}, u32[]{:S(2)}) collective-permute-start(bf16[8,2,1,256,128]{4,3,0,2,1:T(8,128)(2,1)S(1)} %broadcast_select_fusion.3), channel_id=1, source_target_pairs={{0,64},{8,72},{16,80},{24,88},{32,96},{40,104},{48,112},{56,120},{... | collective-permute-start | bytes 3145736 | tf_op jit(solution)/shard_map/ppermute | solution.py:18
  155.3 0.3 fusion.38
  155.5 0.4 copy.122
  156.0 0.6 gather_fusion
  156.5 0.7 convert_reduce_fusion.1
  157.2 21.3 %collective-permute-done.3 = bf16[8,2,1,256,128]{4,3,0,2,1:T(8,128)(2,1)} collective-permute-done((bf16[8,2,1,256,128]{4,3,0,2,1:T(8,128)(2,1)S(1)}, bf16[8,2,1,256,128]{4,3,0,2,1:T(8,128)(2,1)}, u32[]{:S(2)}, u32[]{:S(2)}) %collective-permute-start.3) | collective-permute-done | bytes 1048608 | tf_op jit(solution)/shard_map/ppermute | solution.py:18
  178.6 2.4 broadcast_select_fusion.4
  181.0 6.1 %collective-permute-start.4 = (bf16[8,2,1,256,128]{4,3,0,2,1:T(8,128)(2,1)}, bf16[8,2,1,256,128]{4,3,0,2,1:T(8,128)(2,1)}, u32[]{:S(2)}, u32[]{:S(2)}) collective-permute-start(bf16[8,2,1,256,128]{4,3,0,2,1:T(8,128)(2,1)} %broadcast_select_fusion.4), channel_id=1, source_target_pairs={{0,128},{8,136},{16,144},{24,152},{32,160},{40,168},{48,176},{56,1... | collective-permute-start | bytes 3145736 | tf_op jit(solution)/shard_map/ppermute | solution.py:18
  187.1 0.4 select_reduce_fusion
  187.5 0.7 copy.111
  188.2 0.1 select_reduce_fusion.1
  188.3 0.7 copy.113
  189.0 0.2 convert_reduce_fusion
  189.3 0.1 multiply_reduce_fusion
  189.4 0.2 copy.117
  189.6 0.2 copy.116
  189.7 42.7 %collective-permute-done.4 = bf16[8,2,1,256,128]{4,3,0,2,1:T(8,128)(2,1)} collective-permute-done((bf16[8,2,1,256,128]{4,3,0,2,1:T(8,128)(2,1)}, bf16[8,2,1,256,128]{4,3,0,2,1:T(8,128)(2,1)}, u32[]{:S(2)}, u32[]{:S(2)}) %collective-permute-start.4) | collective-permute-done | bytes 1048608 | tf_op jit(solution)/shard_map/ppermute | solution.py:18
  232.5 1.7 broadcast_select_fusion.5
  234.2 8.5 %collective-permute-start.5 = (bf16[8,2,1,256,128]{4,3,0,2,1:T(8,128)(2,1)S(1)}, bf16[8,2,1,256,128]{4,3,0,2,1:T(8,128)(2,1)}, u32[]{:S(2)}, u32[]{:S(2)}) collective-permute-start(bf16[8,2,1,256,128]{4,3,0,2,1:T(8,128)(2,1)S(1)} %broadcast_select_fusion.5), channel_id=1, source_target_pairs={{0,256},{8,264},{16,272},{24,280},{32,288},{40,296},{48,304},{56,3... | collective-permute-start | bytes 3145736 | tf_op jit(solution)/shard_map/ppermute | solution.py:18
  242.7 0.3 fusion.3
  243.0 0.4 convolution_bitcast_fusion
  243.5 0.1 pad_maximum_fusion
  243.6 3.8 %all_to_all.48 = f32[4,1,1,4,8,130]{5,4,3,2,1,0:T(8,128)S(1)} all-to-all(f32[4,1,1,4,8,130]{5,4,3,2,1,0:T(8,128)S(1)} %copy.118), channel_id=1, replica_groups=mesh['batch'=64,'tensor'=4,'section'=2] {'section'}, dimensions={0} | all-to-all | bytes 133120 | tf_op jit(solution)/shard_map/all_to_all | solution.py:26
  247.4 0.7 copy.119
  248.2 1.1 fusion.4
  249.3 1.8 copy.124
  251.2 37.0 %collective-permute-done.5 = bf16[8,2,1,256,128]{4,3,0,2,1:T(8,128)(2,1)} collective-permute-done((bf16[8,2,1,256,128]{4,3,0,2,1:T(8,128)(2,1)S(1)}, bf16[8,2,1,256,128]{4,3,0,2,1:T(8,128)(2,1)}, u32[]{:S(2)}, u32[]{:S(2)}) %collective-permute-start.5) | collective-permute-done | bytes 1048608 | tf_op jit(solution)/shard_map/ppermute | solution.py:18
  288.1 1.4 select_bitcast_fusion
  289.6 1.0 copy.125
  (48 shorter events, 0.4 us)
Async XLA Ops:
  2.9 4.4 %copy-start.12 = (s32[4,5]{1,0:T(4,128)S(1)}, s32[4,5]{1,0:T(4,128)}, u32[]{:S(2)}) copy-start(s32[4,5]{1,0:T(4,128)} %param.8) | copy-start | bytes 244
  2.9 4.5 %copy-start.14 = (s32[4]{0:T(128)S(1)}, s32[4]{0:T(128)}, u32[]{:S(2)}) copy-start(s32[4]{0:T(128)} %param.7) | copy-start | bytes 52
  2.9 19.5 %all-to-all-start.1 = ((bf16[1,2,2,4,256,128]{5,4,2,1,0,3:T(8,128)(2,1)}), bf16[1,2,2,4,256,128]{5,4,2,1,0,3:T(8,128)(2,1)S(1)}, u32[]{:S(2)}, u32[]{:S(2)}) async-start(bf16[1,2,2,4,256,128]{5,4,2,1,0,3:T(8,128)(2,1)} %copy.109), calls=%async_computation.1 | async-start | bytes 2097152 | tf_op jit(solution)/shard_map/all_to_all | solution.py:63
  22.5 3.4 %copy-start.9 = (s32[64,8]{0,1:T(8,128)S(1)}, s32[64,8]{0,1:T(8,128)}, u32[]{:S(2)}) copy-start(s32[64,8]{0,1:T(8,128)} %param.9) | copy-start | bytes 6148
  22.7 25.7 %collective-permute-start = (bf16[8,2,1,256,128]{4,3,0,2,1:T(8,128)(2,1)S(1)}, bf16[8,2,1,256,128]{4,3,0,2,1:T(8,128)(2,1)S(1)}, u32[]{:S(2)}, u32[]{:S(2)}) collective-permute-start(bf16[8,2,1,256,128]{4,3,0,2,1:T(8,128)(2,1)S(1)} %broadcast_select_fusion), channel_id=1, source_target_pairs={{0,8},{8,0},{16,24},{24,16},{32,40},{40,32},{48,56},{56,48},{64,72... | collective-permute-start | bytes 3145736 | tf_op jit(solution)/shard_map/ppermute | solution.py:18
  48.6 48.2 %collective-permute-start.1 = (bf16[8,2,1,256,128]{4,3,0,2,1:T(8,128)(2,1)S(1)}, bf16[8,2,1,256,128]{4,3,0,2,1:T(8,128)(2,1)S(1)}, u32[]{:S(2)}, u32[]{:S(2)}) collective-permute-start(bf16[8,2,1,256,128]{4,3,0,2,1:T(8,128)(2,1)S(1)} %broadcast_select_fusion.1), channel_id=1, source_target_pairs={{0,16},{8,24},{16,0},{24,8},{32,48},{40,56},{48,32},{56,40},{64,80... | collective-permute-start | bytes 3145736 | tf_op jit(solution)/shard_map/ppermute | solution.py:18
  96.7 4.8 %copy-start.3 = (bf16[2,2,4,8,128]{4,3,2,1,0:T(8,128)(2,1)S(1)}, bf16[2,2,4,8,128]{4,3,2,1,0:T(8,128)(2,1)}, u32[]{:S(2)}) copy-start(bf16[2,2,4,8,128]{4,3,2,1,0:T(8,128)(2,1)} %param.10) | copy-start | bytes 98308
  96.7 8.7 %copy-start.4 = (bf16[2,2,4,2,1,128]{5,3,4,2,1,0:T(2,128)(2,1)S(1)}, bf16[2,2,4,2,1,128]{5,3,4,2,1,0:T(2,128)(2,1)}, u32[]{:S(2)}) copy-start(bf16[2,2,4,2,1,128]{5,3,4,2,1,0:T(2,128)(2,1)} %param.11) | copy-start | bytes 24580
  96.9 52.7 %collective-permute-start.2 = (bf16[8,2,1,256,128]{4,3,0,2,1:T(8,128)(2,1)S(1)}, bf16[8,2,1,256,128]{4,3,0,2,1:T(8,128)(2,1)}, u32[]{:S(2)}, u32[]{:S(2)}) collective-permute-start(bf16[8,2,1,256,128]{4,3,0,2,1:T(8,128)(2,1)S(1)} %broadcast_select_fusion.2), channel_id=1, source_target_pairs={{0,32},{8,40},{16,48},{24,56},{32,0},{40,8},{48,16},{56,24},{64,96... | collective-permute-start | bytes 3145736 | tf_op jit(solution)/shard_map/ppermute | solution.py:18
  102.1 53.8 %all-to-all-start = ((bf16[2,2,4,8,128]{4,3,2,0,1:T(8,128)(2,1)}), bf16[2,2,4,8,128]{4,3,2,0,1:T(8,128)(2,1)S(1)}, u32[]{:S(2)}, u32[]{:S(2)}) async-start(bf16[2,2,4,8,128]{4,3,2,0,1:T(8,128)(2,1)} %copy.108), calls=%async_computation | async-start | bytes 65536 | tf_op jit(solution)/shard_map/all_to_all | solution.py:74
  105.8 50.8 %copy-start = (f32[4,4,8]{2,1,0:T(4,128)}, f32[4,4,8]{2,1,0:T(4,128)S(1)}, u32[]{:S(2)}) copy-start(f32[4,4,8]{2,1,0:T(4,128)S(1)} %get-tuple-element.31) | copy-start | bytes 1540
  151.0 27.6 %collective-permute-start.3 = (bf16[8,2,1,256,128]{4,3,0,2,1:T(8,128)(2,1)S(1)}, bf16[8,2,1,256,128]{4,3,0,2,1:T(8,128)(2,1)}, u32[]{:S(2)}, u32[]{:S(2)}) collective-permute-start(bf16[8,2,1,256,128]{4,3,0,2,1:T(8,128)(2,1)S(1)} %broadcast_select_fusion.3), channel_id=1, source_target_pairs={{0,64},{8,72},{16,80},{24,88},{32,96},{40,104},{48,112},{56,120},{... | collective-permute-start | bytes 3145736 | tf_op jit(solution)/shard_map/ppermute | solution.py:18
  157.2 32.0 %copy-start.10 = (pred[4,8]{1,0:T(4,128)(4,1)}, pred[4,8]{1,0:T(4,128)(4,1)S(1)}, u32[]{:S(2)}) copy-start(pred[4,8]{1,0:T(4,128)(4,1)S(1)} %fusion.20) | copy-start | bytes 100
  181.0 51.5 %collective-permute-start.4 = (bf16[8,2,1,256,128]{4,3,0,2,1:T(8,128)(2,1)}, bf16[8,2,1,256,128]{4,3,0,2,1:T(8,128)(2,1)}, u32[]{:S(2)}, u32[]{:S(2)}) collective-permute-start(bf16[8,2,1,256,128]{4,3,0,2,1:T(8,128)(2,1)} %broadcast_select_fusion.4), channel_id=1, source_target_pairs={{0,128},{8,136},{16,144},{24,152},{32,160},{40,168},{48,176},{56,1... | collective-permute-start | bytes 3145736 | tf_op jit(solution)/shard_map/ppermute | solution.py:18
  187.1 1.9 copy-start.5
  232.5 10.2 %copy-start.6 = (pred[8,256]{1,0:T(8,128)(4,1)S(1)}, pred[8,256]{1,0:T(8,128)(4,1)}, u32[]{:S(2)}) copy-start(pred[8,256]{1,0:T(8,128)(4,1)} %copy-done.5) | copy-start | bytes 6148
  232.5 10.5 %copy-start.7 = (f32[4,4,8]{0,2,1:T(8,128)S(1)}, f32[4,4,8]{0,2,1:T(8,128)}, u32[]{:S(2)}) copy-start(f32[4,4,8]{0,2,1:T(8,128)} %copy.113) | copy-start | bytes 1540
  232.5 10.5 %copy-start.8 = (f32[8,4,8]{0,2,1:T(8,128)S(1)}, f32[8,4,8]{0,2,1:T(8,128)}, u32[]{:S(2)}) copy-start(f32[8,4,8]{0,2,1:T(8,128)} %copy.111) | copy-start | bytes 3076
  232.5 10.5 %copy-start.11 = (pred[4,8]{1,0:T(4,128)(4,1)S(1)}, pred[4,8]{1,0:T(4,128)(4,1)}, u32[]{:S(2)}) copy-start(pred[4,8]{1,0:T(4,128)(4,1)} %copy-done.10) | copy-start | bytes 100
  234.2 53.9 %collective-permute-start.5 = (bf16[8,2,1,256,128]{4,3,0,2,1:T(8,128)(2,1)S(1)}, bf16[8,2,1,256,128]{4,3,0,2,1:T(8,128)(2,1)}, u32[]{:S(2)}, u32[]{:S(2)}) collective-permute-start(bf16[8,2,1,256,128]{4,3,0,2,1:T(8,128)(2,1)S(1)} %broadcast_select_fusion.5), channel_id=1, source_target_pairs={{0,256},{8,264},{16,272},{24,280},{32,288},{40,296},{48,304},{56,3... | collective-permute-start | bytes 3145736 | tf_op jit(solution)/shard_map/ppermute | solution.py:18
  243.4 4.7 %copy-start.1 = (f32[4,4,8]{2,1,0:T(4,128)S(1)}, f32[4,4,8]{2,1,0:T(4,128)}, u32[]{:S(2)}) copy-start(f32[4,4,8]{2,1,0:T(4,128)} %copy-done) | copy-start | bytes 1540
  243.4 4.7 %copy-start.2 = (f32[4,4,8]{2,1,0:T(4,128)S(1)}, f32[4,4,8]{2,1,0:T(4,128)}, u32[]{:S(2)}) copy-start(f32[4,4,8]{2,1,0:T(4,128)} %convert_reduce_fusion.1) | copy-start | bytes 1540
  248.2 40.0 %copy-start.13 = (pred[8]{0:T(512)(128)(4,1)S(1)}, pred[8]{0:T(512)(128)(4,1)}, u32[]{:S(2)}) copy-start(pred[8]{0:T(512)(128)(4,1)} %get-tuple-element.25) | copy-start | bytes 28
where the time goes:
time: 291 us
  waiting for transfers between devices  226 us (78%)
  starting transfers between devices  38.4 us (13%)
  other arithmetic  10.6 us (4%)
  local copies, waits for them, and re-layouts  9.58 us (3%)
  blocking collectives  3.84 us (1%)
    ppermute x6, waiting for transfers between devices, partner_2(): return lax.ppermute(value, axis, pairs)  211 us
    ppermute x6, starting transfers between devices, partner_2(): return lax.ppermute(value, axis, pairs)  30.7 us
    all_to_all x1, waiting for transfers between devices, on_device(): lax.all_to_all(prefill_cache, 'tensor', split_axis=3, concat_axis=1, tile...  14.9 us
    unnamed x37, local copies, waits for them, and re-layouts  5.96 us
    select_n x5, other arithmetic, pick_where(): jnp.where(take.reshape((-1,) + (1,) * (own.ndim - 1)), other, own)  5.86 us
  transfers between devices with their start and end apart: 8, of which 7 were waited for; matrix products, arithmetic and copies ran while one was open for 4% of the time, Pallas kernels for 0%

commit v1 on v0

v1 whole, which is shorter than its diff:
```python
import math

import jax
import jax.numpy as jnp
from jax import lax
from jax.experimental import pallas as pl
from jax.experimental.pallas import tpu as pltpu
from jax.sharding import PartitionSpec as P

MASKED = -1e30


def partner_swap(value, axis, mask):
    pairs = [(source, source ^ mask) for source in range(lax.axis_size(axis))]
    return lax.ppermute(value, axis, pairs)


def page_partials(queries_at, key_rows, value_rows, token_mask):
    score_scale = 1.0 / math.sqrt(key_rows.shape[-1])
    scores = (
        jnp.einsum("nigex,ngpx->ngiep", queries_at, key_rows, preferred_element_type=jnp.float32)
        * score_scale
    )
    page_peak = jnp.max(jnp.where(token_mask, scores, MASKED), axis=-1)
    weights = jnp.where(token_mask, jnp.exp(scores - page_peak[..., None]), 0.0).astype(
        jnp.bfloat16
    )
    weight_sum = jnp.sum(weights.astype(jnp.float32), axis=-1)
    page_output = jnp.einsum(
        "ngiep,ngpx->ngiex", weights, value_rows, preferred_element_type=jnp.float32
    )
    return (page_peak, weight_sum, page_output)


def by_destination(keys, landed):
    batches, slots, heads, rows, width = landed.shape

    def body(keys_ref, landed_ref, out_ref):
        def step(dest, carry):
            for slot in range(slots):
                source = dest ^ keys_ref[slot]
                for head in range(heads):
                    out_ref[dest, head, slot] = landed_ref[source, slot, head]
            return carry

        lax.fori_loop(0, batches, step, 0, unroll=4)

    return pl.pallas_call(
        body,
        out_shape=jax.ShapeDtypeStruct((batches, heads, slots, rows, width), landed.dtype),
        in_specs=[
            pl.BlockSpec(memory_space=pltpu.SMEM),
            pl.BlockSpec(memory_space=pltpu.VMEM),
        ],
        out_specs=pl.BlockSpec(memory_space=pltpu.VMEM),
    )(keys, landed)


def on_device(prefill_cache, lengths, page_table, holder, queries, new_kv):
    batch_count, positions = holder.shape
    tensor_size = lax.axis_size("tensor")
    tensor_at = lax.axis_index("tensor")
    section_at = lax.axis_index("section")
    raw = prefill_cache[0]
    own_slots, kinds, heads, page_len, head_dim = raw.shape
    blocks = batch_count // kinds
    block_rows = page_len // blocks
    owned_rows, layers, step_count = (queries.shape[0], queries.shape[1], queries.shape[2])
    group_size = queries.shape[3]
    req_count, max_pages = page_table.shape

    slot_ids = jnp.arange(positions, dtype=jnp.int32)
    page_hits = (page_table[:, :, None] == slot_ids).astype(jnp.int32)
    in_use = jnp.sum(page_hits, axis=(0, 1)) > 0

    own_use = lax.dynamic_slice(in_use, (tensor_at * own_slots,), (own_slots,))
    own_keys = lax.dynamic_slice(holder[0], (tensor_at * own_slots,), (own_slots,))
    kept = jnp.where(own_use[:, None, None, None, None], raw, jnp.zeros((), raw.dtype))
    pieces = jnp.transpose(
        kept.reshape(own_slots, kinds, heads, blocks, block_rows, head_dim), (1, 3, 0, 2, 4, 5)
    ).reshape(batch_count, own_slots, heads, block_rows, head_dim)
    landed = lax.all_to_all(pieces, "batch", split_axis=0, concat_axis=0, tiled=True)

    outgoing = by_destination(own_keys, landed).reshape(
        batch_count * tensor_size, own_slots, block_rows, head_dim
    )
    arrived = lax.all_to_all(
        outgoing, ("batch", "tensor"), split_axis=0, concat_axis=0, tiled=True
    )
    decode_pool = jnp.transpose(
        arrived.reshape(batch_count, positions, block_rows, head_dim), (1, 0, 2, 3)
    ).reshape(1, positions, kinds, 1, page_len, head_dim)

    def head_of(index):
        return lax.dynamic_index_in_dim(raw, index, 2, keepdims=False)

    page_blocks = [head_of(tensor_at)]
    for mask in range(1, tensor_size):
        page_blocks.append(partner_swap(head_of(tensor_at ^ mask), "tensor", mask))
    local_pages = jnp.concatenate(page_blocks, axis=0)[:, :, None]
    slot_at = jnp.concatenate(
        [
            (tensor_at ^ mask) * own_slots + jnp.arange(own_slots, dtype=jnp.int32)
            for mask in range(tensor_size)
        ]
    )

    theirs = lax.dynamic_index_in_dim(queries, 1 - section_at, 1, keepdims=False)
    mine_q = lax.dynamic_index_in_dim(queries, section_at, 1, keepdims=False)
    got = partner_swap(theirs, "section", 1)
    first = section_at == 0
    local_queries = jnp.concatenate(
        [jnp.where(first, mine_q, got), jnp.where(first, got, mine_q)], axis=0
    ).reshape(req_count, step_count, 1, group_size, head_dim)

    hits = (page_table[:, :, None] == slot_at).astype(jnp.int32)
    used_at = jnp.sum(hits, axis=(0, 1)) > 0
    request_of = jnp.sum(
        hits * jnp.arange(req_count, dtype=jnp.int32)[:, None, None], axis=(0, 1)
    )
    page_of = jnp.sum(hits * jnp.arange(max_pages, dtype=jnp.int32)[None, :, None], axis=(0, 1))
    length_of = jnp.sum(hits * lengths[:, None, None], axis=(0, 1))
    live_count = jnp.clip(length_of - page_of * page_len, 0, page_len)
    position_queries = jnp.take(local_queries, request_of, axis=0)
    token_index = jnp.arange(page_len, dtype=jnp.int32)
    token_mask = token_index[None, None, None, None, :] < live_count[:, None, None, None, None]
    page_peak, weight_sum, page_output = page_partials(
        position_queries, local_pages[:, 0], local_pages[:, 1], token_mask
    )
    mine = (request_of[None, :] == jnp.arange(req_count, dtype=jnp.int32)[:, None]) & used_at[
        None, :
    ]
    row_mask = mine[:, :, None, None, None]
    request_peak = jnp.max(jnp.where(row_mask, page_peak[None], MASKED), axis=1)
    factor = jnp.where(row_mask, jnp.exp(page_peak[None] - request_peak[:, None]), 0.0)
    numerator = jnp.einsum(
        "rqgie,qgiex->rgiex", factor, page_output, precision=lax.Precision.HIGHEST
    )
    denominator = jnp.sum(factor * weight_sum[None], axis=1)

    merged = jnp.concatenate(
        [numerator, request_peak[..., None], denominator[..., None]], axis=-1
    )
    keep = lax.dynamic_slice_in_dim(merged, section_at * owned_rows, owned_rows, 0)
    give = lax.dynamic_slice_in_dim(merged, (1 - section_at) * owned_rows, owned_rows, 0)
    back = partner_swap(give, "section", 1)
    merged = jnp.stack([jnp.where(first, keep, back), jnp.where(first, back, keep)], axis=1)
    numerator = merged[..., :head_dim]
    request_peak = merged[..., head_dim]
    denominator = merged[..., head_dim + 1]

    flat_queries = queries.reshape(owned_rows * layers, step_count, 1, group_size, head_dim)
    new_keys = jnp.transpose(
        new_kv[:, :, :, 0].reshape(owned_rows * layers, step_count, 1, head_dim), (0, 2, 1, 3)
    )
    new_values = jnp.transpose(
        new_kv[:, :, :, 1].reshape(owned_rows * layers, step_count, 1, head_dim), (0, 2, 1, 3)
    )
    step_index = jnp.arange(step_count, dtype=jnp.int32)
    causal = step_index[None, :] <= step_index[:, None]
    new_peak, new_sum, new_output = page_partials(
        flat_queries, new_keys, new_values, causal[None, None, :, None, :]
    )
    new_peak = new_peak.reshape(request_peak.shape)
    new_sum = new_sum.reshape(denominator.shape)
    new_output = new_output.reshape(numerator.shape)
    joint_peak = jnp.maximum(request_peak, new_peak)
    old_scale = jnp.exp(request_peak - joint_peak)
    new_scale = jnp.exp(new_peak - joint_peak)
    result = (old_scale[..., None] * numerator + new_scale[..., None] * new_output) / (
        old_scale * denominator + new_scale * new_sum
    )[..., None]
    attended = (
        jnp.transpose(result, (0, 1, 3, 2, 4, 5))
        .reshape(owned_rows, layers, step_count, group_size, head_dim)
        .astype(jnp.bfloat16)
    )
    return (attended, decode_pool)


def solution(mesh):
    placed = (
        P("section", ("batch", "tensor"), None, None, None, None),
        P("batch"),
        P("batch", None),
        P(),
        P(("batch", "section"), None, None, "tensor", None),
        P(("batch", "section"), None, None, None, "tensor", None),
    )
    return jax.shard_map(
        on_device,
        mesh=mesh,
        in_specs=placed,
        out_specs=(
            P(("batch", "section"), None, None, "tensor", None),
            P("section", "batch", None, "tensor", None, None),
        ),
        check_vma=False,
    )
```

time: 291 us -> 112 us (0.38)
  the two profiles are of different devices: /device:TPU:56 before, /device:TPU:8 now
where the time goes in v1:
time: 112 us; the launch traced here: 111 us
  waiting for transfers between devices  49.6 us (44%)
  starting transfers between devices  43.2 us (39%)
  local copies, waits for them, and re-layouts  9.68 us (9%)
  other arithmetic  3.33 us (3%)
  Pallas kernels  2.58 us (2%)
  matrix products  1.63 us (1%)
  between operations  1.13 us (1%)
    all_to_all x1, waiting for transfers between devices, on_device(): lax.all_to_all(pieces, 'batch', split_axis=0, concat_axis=0, tiled=True)  26.9 us
    all_to_all x1, waiting for transfers between devices, on_device(): lax.all_to_all(outgoing, ('batch', 'tensor'), split_axis=0, concat_axis=0...  22.7 us
    all_to_all x1, starting transfers between devices, on_device(): lax.all_to_all(pieces, 'batch', split_axis=0, concat_axis=0, tiled=True)  16.7 us
    ppermute x5, starting transfers between devices, partner_swap(): return lax.ppermute(value, axis, pairs)  14.4 us
    all_to_all x1, starting transfers between devices, on_device(): lax.all_to_all(outgoing, ('batch', 'tensor'), split_axis=0, concat_axis=0...  12.1 us
    unnamed x24, local copies, waits for them, and re-layouts  3.14 us
    pallas_call x1, Pallas kernels, by_destination(): pl.pallas_call(body, out_shape=jax.ShapeDtypeStruct((batches, heads, slot...  2.58 us
  transfers between devices with their start and end apart: 7, of which 2 were waited for; matrix products, arithmetic and copies ran while one was open for 9% of the time, Pallas kernels for 0%

profile of v1, /device:TPU:8, one launch (start us, length us, event | category | flops | bytes accessed | tf_op | source)
XLA Modules:
  0.0 111.2 jit_solution(11037165729620597362)
XLA Ops:
  0.6 0.0 copy-start
  0.7 1.3 %constant_dynamic-slice_fusion.5 = (bf16[1,2,2,1,256,128]{5,4,3,2,1,0:T(8,128)(2,1)S(1)}, bf16[1,2,2,1,256,128]{5,4,3,2,1,0:T(8,128)(2,1)S(1)}, bf16[1,2,2,1,256...) fusion(bf16[1,2,2,4,256,128]{5,4,3,2,1,0:T(8,128)(2,1)} %param.6, s32[]{:T(128)S(6)} %select_n.137, ...), kind=kLoop, calls=%fused_computation.75 | loop fusion | bytes 2097168 | tf_op jit(solution)/shard_map/jit(dynamic_index_in_dim)/dynamic_slice | solution.py:95
  2.0 0.0 copy-start.7
  2.0 0.0 copy-start.1
  2.0 3.5 %collective-permute-start.1 = (bf16[2,2,256,128]{3,2,0,1:T(8,128)(2,1)S(1)}, bf16[2,2,256,128]{3,2,0,1:T(8,128)(2,1)S(1)}, u32[]{:S(2)}, u32[]{:S(2)}) collective-permute-start(bf16[2,2,256,128]{3,2,0,1:T(8,128)(2,1)S(1)} %bitcast.99), channel_id=1, source_target_pairs={{0,2},{2,0},{4,6},{6,4},{1,3},{3,1},{5,7},{7,5},{8,10},{10,8},{12,... | collective-permute-start | bytes 786440 | tf_op jit(solution)/shard_map/ppermute | solution.py:15
  5.6 4.6 %collective-permute-start.2 = (bf16[2,2,256,128]{3,2,0,1:T(8,128)(2,1)S(1)}, bf16[2,2,256,128]{3,2,0,1:T(8,128)(2,1)S(1)}, u32[]{:S(2)}, u32[]{:S(2)}) collective-permute-start(bf16[2,2,256,128]{3,2,0,1:T(8,128)(2,1)S(1)} %bitcast.100), channel_id=1, source_target_pairs={{0,4},{2,6},{4,0},{6,2},{1,5},{3,7},{5,1},{7,3},{8,12},{10,14},{12... | collective-permute-start | bytes 786440 | tf_op jit(solution)/shard_map/ppermute | solution.py:15
  10.3 2.4 %collective-permute-start.3 = (bf16[2,2,256,128]{3,2,0,1:T(8,128)(2,1)S(1)}, bf16[2,2,256,128]{3,2,0,1:T(8,128)(2,1)S(1)}, u32[]{:S(2)}, u32[]{:S(2)}) collective-permute-start(bf16[2,2,256,128]{3,2,0,1:T(8,128)(2,1)S(1)} %bitcast.101), channel_id=1, source_target_pairs={{0,6},{2,4},{4,2},{6,0},{1,7},{3,5},{5,3},{7,1},{8,14},{10,12},{12... | collective-permute-start | bytes 786440 | tf_op jit(solution)/shard_map/ppermute | solution.py:15
  12.7 1.9 %collective-permute-start = (bf16[2,4,8,128]{3,2,1,0:T(8,128)(2,1)S(1)}, bf16[2,4,8,128]{3,2,1,0:T(8,128)(2,1)S(1)}, u32[]{:S(2)}, u32[]{:S(2)}) collective-permute-start(bf16[2,4,8,128]{3,2,1,0:T(8,128)(2,1)S(1)} %dynamic-slice_bitcast_fusion), channel_id=1, source_target_pairs={{0,1},{1,0},{2,3},{3,2},{4,5},{5,4},{6,7},{7,6},{8,9},{9,8},{10,11... | collective-permute-start | bytes 49160 | tf_op jit(solution)/shard_map/ppermute | solution.py:15
  14.7 0.1 copy.166
  14.8 0.1 pad_add_fusion
  14.9 0.1 fusion.22
  15.0 0.1 dynamic_slice.44
  15.1 1.3 %copy_select_fusion = bf16[2,2,4,32,8,128]{5,4,2,0,3,1:T(8,128)(2,1)} fusion(pred[2]{0:T(512)(128)(4,1)S(1)} %dynamic_slice.44, bf16[1,2,2,4,256,128]{5,4,3,2,1,0:T(8,128)(2,1)S(1)} %copy-done.1), kind=kLoop, calls=%fused_computation.11 | loop fusion | flops 524288 | bytes 2097154 | tf_op jit(solution)/shard_map/jit(_where)/select_n | solution.py:78
  16.4 16.7 %all-to-all-start = ((bf16[64,2,4,8,128]{4,3,2,1,0:T(8,128)(2,1)}), bf16[64,2,4,8,128]{4,3,2,1,0:T(8,128)(2,1)S(1)}, u32[]{:S(2)}, u32[]{:S(2)}) async-start(bf16[64,2,4,8,128]{4,3,2,1,0:T(8,128)(2,1)} %bitcast.39), calls=%async_computation | async-start | bytes 2097152 | tf_op jit(solution)/shard_map/all_to_all | solution.py:82
  33.3 0.1 iota_compare_fusion.1
  33.3 0.3 select_reduce_fusion.2
  33.6 0.0 copy-start.4
  33.6 0.3 fusion.36
  33.9 0.7 fusion.31.keys_ref
  34.7 0.6 gather_fusion
  35.3 0.1 maximum_bitcast_fusion
  35.4 0.4 select_reduce_fusion
  35.8 0.1 copy.171
  35.9 0.3 fusion.5
  36.2 26.9 %all-to-all-done.landed_ref = bf16[64,2,4,8,128]{4,3,2,1,0:T(8,128)(2,1)S(1)} async-done(((bf16[64,2,4,8,128]{4,3,2,1,0:T(8,128)(2,1)}), bf16[64,2,4,8,128]{4,3,2,1,0:T(8,128)(2,1)S(1)}, u32[]{:S(2)}, u32[]{:S(2)}) %all-to-all-start) | async-done | bytes 1048608 | tf_op jit(solution)/shard_map/all_to_all | solution.py:82
  63.1 1.0 copy-done.2
  64.1 2.6 %shard_map.77 = bf16[64,4,2,8,128]{4,3,2,1,0:T(8,128)(2,1)} custom-call(s32[2]{0:T(128)} %fusion.31.keys_ref, bf16[64,2,4,8,128]{4,3,2,1,0:T(8,128)(2,1)} %copy-done.2), custom_call_target="tpu_custom_call" | custom-call | tf_op jit(solution)/shard_map/pallas_call | solution.py:48
  66.6 12.1 %all-to-all-start.1 = ((bf16[256,2,8,128]{3,2,1,0:T(8,128)(2,1)}), bf16[256,2,8,128]{3,2,1,0:T(8,128)(2,1)S(1)}, u32[]{:S(2)}, u32[]{:S(2)}) async-start(bf16[256,2,8,128]{3,2,1,0:T(8,128)(2,1)} %bitcast.93), calls=%async_computation.1 | async-start | bytes 2097152 | tf_op jit(solution)/shard_map/all_to_all | solution.py:87
  78.7 0.1 select_reduce_fusion.1
  78.8 0.1 copy.173
  78.9 0.4 fusion.7
  79.4 0.4 copy.175
  79.8 0.2 convert_reduce_fusion
  80.0 0.1 multiply_reduce_fusion
  80.1 0.3 pad_maximum_fusion
  80.4 0.0 copy-start.5
  80.5 0.3 copy.179
  80.8 1.9 %collective-permute-start.4 = (f32[2,1,4,8,130]{4,3,2,1,0:T(8,128)S(1)}, f32[2,1,4,8,130]{4,3,2,1,0:T(8,128)S(1)}, u32[]{:S(2)}, u32[]{:S(2)}) collective-permute-start(f32[2,1,4,8,130]{4,3,2,1,0:T(8,128)S(1)} %copy.179), channel_id=1, source_target_pairs={{0,1},{1,0},{2,3},{3,2},{4,5},{5,4},{6,7},{7,6},{8,9},{9,8},{10,11... | collective-permute-start | bytes 99848 | tf_op jit(solution)/shard_map/ppermute | solution.py:15
  82.8 0.1 convert_reduce_fusion.1
  82.9 1.3 %copy.185 = f32[2,2,1,4,8,128]{4,3,5,2,1,0:T(4,128)} copy(f32[2,2,1,4,8,128]{5,4,3,1,0,2:T(8,128)S(1)} %bitcast.98) | data formatting | bytes 131072 | tf_op jit(solution)/shard_map/reshape | solution.py:166
  84.2 0.4 copy.180
  84.6 0.2 select_bitcast_fusion.1
  84.8 0.0 copy-start.3
  84.8 1.2 %copy-done.3 = f32[2,2,1,4,8,128]{4,3,5,2,1,0:T(4,128)S(1)} copy-done((f32[2,2,1,4,8,128]{4,3,5,2,1,0:T(4,128)S(1)}, f32[2,2,1,4,8,128]{4,3,5,2,1,0:T(4,128)}, u32[]{:S(2)}) %copy-start.3) | copy-done | bytes 65560
  86.0 0.5 fusion.6
  86.5 0.8 copy.189
  87.3 22.7 %all-to-all-done.1 = bf16[256,2,8,128]{3,2,1,0:T(8,128)(2,1)S(1)} async-done(((bf16[256,2,8,128]{3,2,1,0:T(8,128)(2,1)}), bf16[256,2,8,128]{3,2,1,0:T(8,128)(2,1)S(1)}, u32[]{:S(2)}, u32[]{:S(2)}) %all-to-all-start.1) | async-done | bytes 1048608 | tf_op jit(solution)/shard_map/all_to_all | solution.py:87
  110.0 1.2 %copy.188 = bf16[64,8,8,128]{3,2,0,1:T(8,128)(2,1)} copy(bf16[64,8,8,128]{3,2,1,0:T(8,128)(2,1)S(1)} %bitcast.94) | data formatting | bytes 2097152 | tf_op jit(solution)/shard_map/reshape | solution.py:91
  (43 shorter events, 0.3 us)
Async XLA Ops:
  0.6 33.3 %copy-start = (s32[64,8]{0,1:T(8,128)S(1)}, s32[64,8]{0,1:T(8,128)}, u32[]{:S(2)}) copy-start(s32[64,8]{0,1:T(8,128)} %param.9) | copy-start | bytes 6148
  2.0 10.7 %copy-start.7 = (bf16[2,2,4,8,128]{4,3,2,1,0:T(8,128)(2,1)S(1)}, bf16[2,2,4,8,128]{4,3,2,1,0:T(8,128)(2,1)}, u32[]{:S(2)}) copy-start(bf16[2,2,4,8,128]{4,3,2,1,0:T(8,128)(2,1)} %param.10) | copy-start | bytes 98308
  2.0 12.7 %copy-start.8 = (s32[4,5]{1,0:T(4,128)S(1)}, s32[4,5]{1,0:T(4,128)}, u32[]{:S(2)}) copy-start(s32[4,5]{1,0:T(4,128)} %param.8) | copy-start | bytes 244
  2.0 12.9 %copy-start.9 = (s32[4]{0:T(128)S(1)}, s32[4]{0:T(128)}, u32[]{:S(2)}) copy-start(s32[4]{0:T(128)} %param.7) | copy-start | bytes 52
  2.0 13.1 %copy-start.1 = (bf16[1,2,2,4,256,128]{5,4,3,2,1,0:T(8,128)(2,1)S(1)}, bf16[1,2,2,4,256,128]{5,4,3,2,1,0:T(8,128)(2,1)}, u32[]{:S(2)}) copy-start(bf16[1,2,2,4,256,128]{5,4,3,2,1,0:T(8,128)(2,1)} %param.6) | copy-start | bytes 3145732
  2.0 33.2 %collective-permute-start.1 = (bf16[2,2,256,128]{3,2,0,1:T(8,128)(2,1)S(1)}, bf16[2,2,256,128]{3,2,0,1:T(8,128)(2,1)S(1)}, u32[]{:S(2)}, u32[]{:S(2)}) collective-permute-start(bf16[2,2,256,128]{3,2,0,1:T(8,128)(2,1)S(1)} %bitcast.99), channel_id=1, source_target_pairs={{0,2},{2,0},{4,6},{6,4},{1,3},{3,1},{5,7},{7,5},{8,10},{10,8},{12,... | collective-permute-start | bytes 786440 | tf_op jit(solution)/shard_map/ppermute | solution.py:15
  5.6 29.7 %collective-permute-start.2 = (bf16[2,2,256,128]{3,2,0,1:T(8,128)(2,1)S(1)}, bf16[2,2,256,128]{3,2,0,1:T(8,128)(2,1)S(1)}, u32[]{:S(2)}, u32[]{:S(2)}) collective-permute-start(bf16[2,2,256,128]{3,2,0,1:T(8,128)(2,1)S(1)} %bitcast.100), channel_id=1, source_target_pairs={{0,4},{2,6},{4,0},{6,2},{1,5},{3,7},{5,1},{7,3},{8,12},{10,14},{12... | collective-permute-start | bytes 786440 | tf_op jit(solution)/shard_map/ppermute | solution.py:15
  10.3 25.0 %collective-permute-start.3 = (bf16[2,2,256,128]{3,2,0,1:T(8,128)(2,1)S(1)}, bf16[2,2,256,128]{3,2,0,1:T(8,128)(2,1)S(1)}, u32[]{:S(2)}, u32[]{:S(2)}) collective-permute-start(bf16[2,2,256,128]{3,2,0,1:T(8,128)(2,1)S(1)} %bitcast.101), channel_id=1, source_target_pairs={{0,6},{2,4},{4,2},{6,0},{1,7},{3,5},{5,3},{7,1},{8,14},{10,12},{12... | collective-permute-start | bytes 786440 | tf_op jit(solution)/shard_map/ppermute | solution.py:15
  12.7 21.9 %collective-permute-start = (bf16[2,4,8,128]{3,2,1,0:T(8,128)(2,1)S(1)}, bf16[2,4,8,128]{3,2,1,0:T(8,128)(2,1)S(1)}, u32[]{:S(2)}, u32[]{:S(2)}) collective-permute-start(bf16[2,4,8,128]{3,2,1,0:T(8,128)(2,1)S(1)} %dynamic-slice_bitcast_fusion), channel_id=1, source_target_pairs={{0,1},{1,0},{2,3},{3,2},{4,5},{5,4},{6,7},{7,6},{8,9},{9,8},{10,11... | collective-permute-start | bytes 49160 | tf_op jit(solution)/shard_map/ppermute | solution.py:15
  16.4 16.8 %copy-start.6 = (bf16[2,2,4,2,1,128]{5,3,4,2,1,0:T(2,128)(2,1)S(1)}, bf16[2,2,4,2,1,128]{5,3,4,2,1,0:T(2,128)(2,1)}, u32[]{:S(2)}) copy-start(bf16[2,2,4,2,1,128]{5,3,4,2,1,0:T(2,128)(2,1)} %param.11) | copy-start | bytes 24580
  16.4 46.7 %all-to-all-start = ((bf16[64,2,4,8,128]{4,3,2,1,0:T(8,128)(2,1)}), bf16[64,2,4,8,128]{4,3,2,1,0:T(8,128)(2,1)S(1)}, u32[]{:S(2)}, u32[]{:S(2)}) async-start(bf16[64,2,4,8,128]{4,3,2,1,0:T(8,128)(2,1)} %bitcast.39), calls=%async_computation | async-start | bytes 2097152 | tf_op jit(solution)/shard_map/all_to_all | solution.py:82
  33.6 1.8 %copy-start.4 = (f32[4,4,8,4]{2,3,1,0:T(4,128)}, f32[4,4,8,4]{2,3,1,0:T(4,128)S(1)}, u32[]{:S(2)}) copy-start(f32[4,4,8,4]{2,3,1,0:T(4,128)S(1)} %get-tuple-element.36) | copy-start | bytes 6148
  63.1 1.0 copy-start.2
  66.6 43.4 %all-to-all-start.1 = ((bf16[256,2,8,128]{3,2,1,0:T(8,128)(2,1)}), bf16[256,2,8,128]{3,2,1,0:T(8,128)(2,1)S(1)}, u32[]{:S(2)}, u32[]{:S(2)}) async-start(bf16[256,2,8,128]{3,2,1,0:T(8,128)(2,1)} %bitcast.93), calls=%async_computation.1 | async-start | bytes 2097152 | tf_op jit(solution)/shard_map/all_to_all | solution.py:87
  80.4 2.3 %copy-start.5 = (f32[4,4,8,4]{2,3,1,0:T(4,128)S(1)}, f32[4,4,8,4]{2,3,1,0:T(4,128)}, u32[]{:S(2)}) copy-start(f32[4,4,8,4]{2,3,1,0:T(4,128)} %copy-done.4) | copy-start | bytes 6148
  80.8 3.4 %collective-permute-start.4 = (f32[2,1,4,8,130]{4,3,2,1,0:T(8,128)S(1)}, f32[2,1,4,8,130]{4,3,2,1,0:T(8,128)S(1)}, u32[]{:S(2)}, u32[]{:S(2)}) collective-permute-start(f32[2,1,4,8,130]{4,3,2,1,0:T(8,128)S(1)} %copy.179), channel_id=1, source_target_pairs={{0,1},{1,0},{2,3},{3,2},{4,5},{5,4},{6,7},{7,6},{8,9},{9,8},{10,11... | collective-permute-start | bytes 99848 | tf_op jit(solution)/shard_map/ppermute | solution.py:15
  84.8 1.2 %copy-start.3 = (f32[2,2,1,4,8,128]{4,3,5,2,1,0:T(4,128)S(1)}, f32[2,2,1,4,8,128]{4,3,5,2,1,0:T(4,128)}, u32[]{:S(2)}) copy-start(f32[2,2,1,4,8,128]{4,3,5,2,1,0:T(4,128)} %copy.185) | copy-start | bytes 196612

commit v2 on v1

--- a/solution.py
+++ b/solution.py
@@ -6,6 +6,7 @@
 from jax.experimental import pallas as pl
 from jax.experimental.pallas import tpu as pltpu
 from jax.sharding import PartitionSpec as P
+
 
 MASKED = -1e30
 
@@ -53,7 +54,56 @@
             pl.BlockSpec(memory_space=pltpu.VMEM),
         ],
         out_specs=pl.BlockSpec(memory_space=pltpu.VMEM),
+        compiler_params=pltpu.CompilerParams(vmem_limit_bytes=4 * 2**20),
     )(keys, landed)
+
+
+def pieces_to_spread(raw, page_table, blocks):
+    slots, kinds, heads, page_len, width = raw.shape
+    rows = page_len // blocks
+    req_count, max_pages = page_table.shape
+    parts = 2
+    step_blocks = blocks // parts
+
+    def body(table_ref, raw_ref, out_ref):
+        first_slot = lax.axis_index("tensor") * slots
+        for slot in range(slots):
+            used = jnp.int32(0)
+            for row in range(req_count):
+                for column in range(max_pages):
+                    hit = table_ref[row, column] == first_slot + slot
+                    used = jnp.where(hit, jnp.int32(1), used)
+
+            @pl.when(used > 0)
+            def copy():
+                for block in range(step_blocks):
+                    for head in range(heads):
+                        out_ref[block, slot, head] = raw_ref[
+                            slot, 0, head, pl.ds(block * rows, rows)
+                        ]
+
+            @pl.when(used == 0)
+            def clear():
+                for block in range(step_blocks):
+                    for head in range(heads):
+                        out_ref[block, slot, head] = jnp.zeros((rows, width), raw.dtype)
+
+    return pl.pallas_call(
+        body,
+        grid=(kinds, parts),
+        out_shape=jax.ShapeDtypeStruct((kinds * blocks, slots, heads, rows, width), raw.dtype),
+        in_specs=[
+            pl.BlockSpec(memory_space=pltpu.SMEM),
+            pl.BlockSpec(
+                (slots, 1, heads, page_len // parts, width), lambda kind, part: (0, kind, 0, part, 0)
+            ),
+        ],
+        out_specs=pl.BlockSpec(
+            (step_blocks, slots, heads, rows, width),
+            lambda kind, part: (kind * parts + part, 0, 0, 0, 0),
+        ),
+        compiler_params=pltpu.CompilerParams(vmem_limit_bytes=4 * 2**20),
+    )(page_table, raw)
 
 
 def on_device(prefill_cache, lengths, page_table, holder, queries, new_kv):
@@ -62,34 +112,16 @@
     tensor_at = lax.axis_index("tensor")
     section_at = lax.axis_index("section")
     raw = prefill_cache[0]
-    own_slots, kinds, heads, page_len, head_dim = raw.shape
+    own_slots, kinds, _, page_len, head_dim = raw.shape
     blocks = batch_count // kinds
     block_rows = page_len // blocks
     owned_rows, layers, step_count = (queries.shape[0], queries.shape[1], queries.shape[2])
     group_size = queries.shape[3]
     req_count, max_pages = page_table.shape
 
-    slot_ids = jnp.arange(positions, dtype=jnp.int32)
-    page_hits = (page_table[:, :, None] == slot_ids).astype(jnp.int32)
-    in_use = jnp.sum(page_hits, axis=(0, 1)) > 0
-
-    own_use = lax.dynamic_slice(in_use, (tensor_at * own_slots,), (own_slots,))
     own_keys = lax.dynamic_slice(holder[0], (tensor_at * own_slots,), (own_slots,))
-    kept = jnp.where(own_use[:, None, None, None, None], raw, jnp.zeros((), raw.dtype))
-    pieces = jnp.transpose(
-        kept.reshape(own_slots, kinds, heads, blocks, block_rows, head_dim), (1, 3, 0, 2, 4, 5)
-    ).reshape(batch_count, own_slots, heads, block_rows, head_dim)
+    pieces = pieces_to_spread(raw, page_table, blocks)
     landed = lax.all_to_all(pieces, "batch", split_axis=0, concat_axis=0, tiled=True)
-
-    outgoing = by_destination(own_keys, landed).reshape(
-        batch_count * tensor_size, own_slots, block_rows, head_dim
-    )
-    arrived = lax.all_to_all(
-        outgoing, ("batch", "tensor"), split_axis=0, concat_axis=0, tiled=True
-    )
-    decode_pool = jnp.transpose(
-        arrived.reshape(batch_count, positions, block_rows, head_dim), (1, 0, 2, 3)
-    ).reshape(1, positions, kinds, 1, page_len, head_dim)
 
     def head_of(index):
         return lax.dynamic_index_in_dim(raw, index, 2, keepdims=False)
@@ -97,6 +129,9 @@
     page_blocks = [head_of(tensor_at)]
     for mask in range(1, tensor_size):
         page_blocks.append(partner_swap(head_of(tensor_at ^ mask), "tensor", mask))
+    outgoing = by_destination(own_keys, landed).reshape(
+        batch_count * tensor_size, own_slots, block_rows, head_dim
+    )
     local_pages = jnp.concatenate(page_blocks, axis=0)[:, :, None]
     slot_at = jnp.concatenate(
         [
@@ -175,6 +210,11 @@
         .reshape(owned_rows, layers, step_count, group_size, head_dim)
         .astype(jnp.bfloat16)
     )
+
+    arrived = lax.all_to_all(outgoing, ("batch", "tensor"), split_axis=0, concat_axis=0, tiled=True)
+    decode_pool = jnp.transpose(
+        arrived.reshape(batch_count, positions, block_rows, head_dim), (1, 0, 2, 3)
+    ).reshape(1, positions, kinds, 1, page_len, head_dim)
     return (attended, decode_pool)
 
 
@@ -187,6 +227,7 @@
         P(("batch", "section"), None, None, "tensor", None),
         P(("batch", "section"), None, None, None, "tensor", None),
     )
+
     return jax.shard_map(
         on_device,
         mesh=mesh,

time: 112 us -> 111 us (level)
  local copies, waits for them, and re-layouts: 9.68 us -> 6.68 us
  Pallas kernels: 2.58 us -> 4.27 us
    pallas_call x0 -> x1, Pallas kernels: none -> 2.41 us  [pieces_to_spread(): pl.pallas_call(body, grid=(kinds, parts), out_shape=jax.ShapeDtypeStruct(...]
    unnamed x24 -> x16, local copies, waits for them, and re-layouts: 3.14 us -> 0.99 us
    select_n x1 -> x0, other arithmetic: 1.34 us -> none  [on_device(): jnp.where(own_use[:, None, None, None, None], raw, jnp.zeros((), raw.dtype))]
  transfers between devices with their start and end apart: 7 -> 7, of which waited for: 2 -> 3; matrix products, arithmetic and copies ran while one was open for 9% -> 9% of each run, Pallas kernels for 0% -> 2%
where the time goes in v2:
time: 111 us; the launch traced here: 110 us
  waiting for transfers between devices  49.1 us (44%)
  starting transfers between devices  43.2 us (39%)
  local copies, waits for them, and re-layouts  6.68 us (6%)
  Pallas kernels  4.27 us (4%)
  other arithmetic  4.13 us (4%)
  matrix products  1.63 us (1%)
    all_to_all x1, waiting for transfers between devices, on_device(): lax.all_to_all(pieces, 'batch', split_axis=0, concat_axis=0, tiled=True)  26.2 us
    all_to_all x1, waiting for transfers between devices, on_device(): lax.all_to_all(outgoing, ('batch', 'tensor'), split_axis=0, concat_axis=0...  22.2 us
    all_to_all x1, starting transfers between devices, on_device(): lax.all_to_all(pieces, 'batch', split_axis=0, concat_axis=0, tiled=True)  16.7 us
    ppermute x5, starting transfers between devices, partner_swap(): return lax.ppermute(value, axis, pairs)  14.4 us
    all_to_all x1, starting transfers between devices, on_device(): lax.all_to_all(outgoing, ('batch', 'tensor'), split_axis=0, concat_axis=0...  12.1 us
    pallas_call x1, Pallas kernels, pieces_to_spread(): pl.pallas_call(body, grid=(kinds, parts), out_shape=jax.ShapeDtypeStruct(...  2.41 us
  transfers between devices with their start and end apart: 7, of which 3 were waited for; matrix products, arithmetic and copies ran while one was open for 9% of the time, Pallas kernels for 2%

profile of v2, /device:TPU:8, one launch (start us, length us, event | category | flops | bytes accessed | tf_op | source)
XLA Modules:
  0.0 110.1 jit_solution(13583870464050871321)
XLA Ops:
  0.6 0.0 copy-start
  0.7 1.3 %constant_dynamic-slice_fusion.5 = (bf16[1,2,2,1,256,128]{5,4,3,2,1,0:T(8,128)(2,1)S(1)}, bf16[1,2,2,1,256,128]{5,4,3,2,1,0:T(8,128)(2,1)S(1)}, bf16[1,2,2,1,256...) fusion(bf16[1,2,2,4,256,128]{5,4,3,2,1,0:T(8,128)(2,1)} %param.6, s32[]{:T(128)S(6)} %select_n.131, ...), kind=kLoop, calls=%fused_computation.72 | loop fusion | bytes 2097168 | tf_op jit(solution)/shard_map/jit(dynamic_index_in_dim)/dynamic_slice | solution.py:127
  2.0 0.0 copy-start.4
  2.0 0.0 copy-start.1
  2.0 0.0 copy-start.2
  2.0 3.5 %collective-permute-start.1 = (bf16[2,2,256,128]{3,2,0,1:T(8,128)(2,1)S(1)}, bf16[2,2,256,128]{3,2,0,1:T(8,128)(2,1)S(1)}, u32[]{:S(2)}, u32[]{:S(2)}) collective-permute-start(bf16[2,2,256,128]{3,2,0,1:T(8,128)(2,1)S(1)} %bitcast.94), channel_id=1, source_target_pairs={{0,2},{2,0},{4,6},{6,4},{1,3},{3,1},{5,7},{7,5},{8,10},{10,8},{12,... | collective-permute-start | bytes 786440 | tf_op jit(solution)/shard_map/ppermute | solution.py:16
  5.6 4.6 %collective-permute-start.2 = (bf16[2,2,256,128]{3,2,0,1:T(8,128)(2,1)S(1)}, bf16[2,2,256,128]{3,2,0,1:T(8,128)(2,1)}, u32[]{:S(2)}, u32[]{:S(2)}) collective-permute-start(bf16[2,2,256,128]{3,2,0,1:T(8,128)(2,1)S(1)} %bitcast.95), channel_id=1, source_target_pairs={{0,4},{2,6},{4,0},{6,2},{1,5},{3,7},{5,1},{7,3},{8,12},{10,14},{12... | collective-permute-start | bytes 786440 | tf_op jit(solution)/shard_map/ppermute | solution.py:16
  10.3 2.4 %collective-permute-start.3 = (bf16[2,2,256,128]{3,2,0,1:T(8,128)(2,1)S(1)}, bf16[2,2,256,128]{3,2,0,1:T(8,128)(2,1)}, u32[]{:S(2)}, u32[]{:S(2)}) collective-permute-start(bf16[2,2,256,128]{3,2,0,1:T(8,128)(2,1)S(1)} %bitcast.96), channel_id=1, source_target_pairs={{0,6},{2,4},{4,2},{6,0},{1,7},{3,5},{5,3},{7,1},{8,14},{10,12},{12... | collective-permute-start | bytes 786440 | tf_op jit(solution)/shard_map/ppermute | solution.py:16
  12.7 1.9 %collective-permute-start = (bf16[2,4,8,128]{3,2,1,0:T(8,128)(2,1)S(1)}, bf16[2,4,8,128]{3,2,1,0:T(8,128)(2,1)S(1)}, u32[]{:S(2)}, u32[]{:S(2)}) collective-permute-start(bf16[2,4,8,128]{3,2,1,0:T(8,128)(2,1)S(1)} %dynamic-slice_bitcast_fusion), channel_id=1, source_target_pairs={{0,1},{1,0},{2,3},{3,2},{4,5},{5,4},{6,7},{7,6},{8,9},{9,8},{10,11... | collective-permute-start | bytes 49160 | tf_op jit(solution)/shard_map/ppermute | solution.py:16
  14.6 2.4 %shard_map.77 = bf16[64,2,4,8,128]{4,3,2,1,0:T(8,128)(2,1)} custom-call(s32[4,5]{1,0:T(4,128)S(1)} %copy-done.2, bf16[2,2,4,256,128]{4,3,2,1,0:T(8,128)(2,1)S(1)} %bitcast.88), custom_call_target="tpu_custom_call" | custom-call | tf_op jit(solution)/shard_map/pallas_call | solution.py:91
  17.0 16.7 %all-to-all-start = ((bf16[64,2,4,8,128]{4,3,2,1,0:T(8,128)(2,1)}), bf16[64,2,4,8,128]{4,3,2,1,0:T(8,128)(2,1)S(1)}, u32[]{:S(2)}, u32[]{:S(2)}) async-start(bf16[64,2,4,8,128]{4,3,2,1,0:T(8,128)(2,1)} %shard_map.77), calls=%async_computation | async-start | bytes 2097152 | tf_op jit(solution)/shard_map/all_to_all | solution.py:124
  33.8 0.1 copy.159
  33.9 0.1 pad_add_fusion
  34.0 0.1 fusion.22
  34.2 0.1 iota_compare_fusion
  34.3 0.3 select_reduce_fusion.2
  34.5 0.3 fusion.36
  34.8 0.1 fusion.31.keys_ref
  35.0 0.0 collective-permute-done
  35.0 0.6 gather_fusion
  35.6 0.0 collective-permute-done.1
  35.6 0.0 collective-permute-done.2
  35.6 0.0 collective-permute-done.3
  35.6 1.2 %maximum_bitcast_fusion = bf16[8,2,1,256,128]{4,3,0,2,1:T(8,128)(2,1)S(1)} fusion(bf16[2,2,256,128]{3,2,0,1:T(8,128)(2,1)} %collective-permute-done.3, bf16[2,2,256,128]{3,2,0,1:T(8,128)(2,1)} %collective-permute-done.2, bf16[2,2,256,128]{3,2,0,1:T(8,128)(2,1)S(1)} %collective-permute-done.1, bf16[2,2,256,128]{3,2,0,1:T(8,128)(2,1)S(1)} %bitcast.92), kind=kLoop, calls=%fused_computation.10 | loop fusion | flops 1572864 | bytes 2097152 | tf_op jit(solution)/shard_map/broadcast_in_dim | solution.py:135
  36.8 0.4 select_reduce_fusion
  37.2 0.1 copy.164
  37.3 0.3 fusion.5
  37.5 26.2 %all-to-all-done.landed_ref = bf16[64,2,4,8,128]{4,3,2,1,0:T(8,128)(2,1)S(1)} async-done(((bf16[64,2,4,8,128]{4,3,2,1,0:T(8,128)(2,1)}), bf16[64,2,4,8,128]{4,3,2,1,0:T(8,128)(2,1)S(1)}, u32[]{:S(2)}, u32[]{:S(2)}) %all-to-all-start) | async-done | bytes 1048608 | tf_op jit(solution)/shard_map/all_to_all | solution.py:124
  63.7 1.9 %shard_map.78 = bf16[64,4,2,8,128]{4,3,2,1,0:T(8,128)(2,1)} custom-call(s32[2]{0:T(128)S(1)} %fusion.31.keys_ref, bf16[64,2,4,8,128]{4,3,2,1,0:T(8,128)(2,1)S(1)} %all-to-all-done.landed_ref), custom_call_target="tpu_custom_call" | custom-call | tf_op jit(solution)/shard_map/pallas_call | solution.py:49
  65.6 12.1 %all-to-all-start.1 = ((bf16[256,2,8,128]{3,2,1,0:T(8,128)(2,1)}), bf16[256,2,8,128]{3,2,1,0:T(8,128)(2,1)S(1)}, u32[]{:S(2)}, u32[]{:S(2)}) async-start(bf16[256,2,8,128]{3,2,1,0:T(8,128)(2,1)} %bitcast.38), calls=%async_computation.1 | async-start | bytes 2097152 | tf_op jit(solution)/shard_map/all_to_all | solution.py:214
  77.7 0.1 select_reduce_fusion.1
  77.8 0.1 copy.166
  77.9 0.4 fusion.7
  78.3 0.4 copy.168
  78.7 0.2 convert_reduce_fusion
  79.0 0.1 multiply_reduce_fusion
  79.1 0.3 pad_maximum_fusion
  79.4 0.3 copy.172
  79.7 1.9 %collective-permute-start.4 = (f32[2,1,4,8,130]{4,3,2,1,0:T(8,128)S(1)}, f32[2,1,4,8,130]{4,3,2,1,0:T(8,128)S(1)}, u32[]{:S(2)}, u32[]{:S(2)}) collective-permute-start(f32[2,1,4,8,130]{4,3,2,1,0:T(8,128)S(1)} %copy.172), channel_id=1, source_target_pairs={{0,1},{1,0},{2,3},{3,2},{4,5},{5,4},{6,7},{7,6},{8,9},{9,8},{10,11... | collective-permute-start | bytes 99848 | tf_op jit(solution)/shard_map/ppermute | solution.py:16
  81.7 0.1 convert_reduce_fusion.1
  81.8 0.4 copy.178
  82.2 0.7 collective-permute-done.4
  82.9 1.1 %copy.173 = f32[2,1,4,8,130]{3,2,4,0,1:T(4,128)} copy(f32[2,1,4,8,130]{4,3,2,1,0:T(8,128)S(1)} %collective-permute-done.4) | data formatting | bytes 66560 | tf_op jit(solution)/shard_map/ppermute | solution.py:16
  84.0 1.3 %select_bitcast_fusion.1 = (f32[2,1,1,4,8,130]{4,3,5,2,1,0:T(4,128)S(1)}, f32[2,1,1,4,8,130]{4,3,5,2,1,0:T(4,128)S(1)}) fusion(f32[2,1,4,8,130]{3,2,4,0,1:T(4,128)} %copy.173, f32[4,1,4,8,130]{3,2,4,0,1:T(4,128)S(1)} %pad_maximum_fusion, s32[]{:T(128)S(6)} %select_n.140, pred[]{:T(512)S(6)} %eq.33), kind=kLoop, calls=%fused_computation.13 | loop fusion | flops 16640 | bytes 133125 | tf_op jit(solution)/shard_map/stack | solution.py:182
  85.4 0.5 fusion.6
  85.9 0.8 copy.181
  86.7 22.2 %all-to-all-done.1 = bf16[256,2,8,128]{3,2,1,0:T(8,128)(2,1)S(1)} async-done(((bf16[256,2,8,128]{3,2,1,0:T(8,128)(2,1)}), bf16[256,2,8,128]{3,2,1,0:T(8,128)(2,1)S(1)}, u32[]{:S(2)}, u32[]{:S(2)}) %all-to-all-start.1) | async-done | bytes 1048608 | tf_op jit(solution)/shard_map/all_to_all | solution.py:214
  108.9 1.2 %copy.180 = bf16[64,8,8,128]{3,2,0,1:T(8,128)(2,1)} copy(bf16[64,8,8,128]{3,2,1,0:T(8,128)(2,1)S(1)} %bitcast.89) | data formatting | bytes 2097152 | tf_op jit(solution)/shard_map/reshape | solution.py:216
  (33 shorter events, 0.3 us)
Async XLA Ops:
  0.6 34.2 %copy-start = (s32[64,8]{0,1:T(8,128)S(1)}, s32[64,8]{0,1:T(8,128)}, u32[]{:S(2)}) copy-start(s32[64,8]{0,1:T(8,128)} %param.9) | copy-start | bytes 6148
  2.0 10.7 %copy-start.4 = (bf16[2,2,4,8,128]{4,3,2,1,0:T(8,128)(2,1)S(1)}, bf16[2,2,4,8,128]{4,3,2,1,0:T(8,128)(2,1)}, u32[]{:S(2)}) copy-start(bf16[2,2,4,8,128]{4,3,2,1,0:T(8,128)(2,1)} %param.10) | copy-start | bytes 98308
  2.0 12.6 %copy-start.1 = (bf16[1,2,2,4,256,128]{5,4,3,2,1,0:T(8,128)(2,1)S(1)}, bf16[1,2,2,4,256,128]{5,4,3,2,1,0:T(8,128)(2,1)}, u32[]{:S(2)}) copy-start(bf16[1,2,2,4,256,128]{5,4,3,2,1,0:T(8,128)(2,1)} %param.6) | copy-start | bytes 3145732
  2.0 12.6 %copy-start.2 = (s32[4,5]{1,0:T(4,128)S(1)}, s32[4,5]{1,0:T(4,128)}, u32[]{:S(2)}) copy-start(s32[4,5]{1,0:T(4,128)} %table_ref.1) | copy-start | bytes 244
  2.0 33.6 %collective-permute-start.1 = (bf16[2,2,256,128]{3,2,0,1:T(8,128)(2,1)S(1)}, bf16[2,2,256,128]{3,2,0,1:T(8,128)(2,1)S(1)}, u32[]{:S(2)}, u32[]{:S(2)}) collective-permute-start(bf16[2,2,256,128]{3,2,0,1:T(8,128)(2,1)S(1)} %bitcast.94), channel_id=1, source_target_pairs={{0,2},{2,0},{4,6},{6,4},{1,3},{3,1},{5,7},{7,5},{8,10},{10,8},{12,... | collective-permute-start | bytes 786440 | tf_op jit(solution)/shard_map/ppermute | solution.py:16
  5.6 30.0 %collective-permute-start.2 = (bf16[2,2,256,128]{3,2,0,1:T(8,128)(2,1)S(1)}, bf16[2,2,256,128]{3,2,0,1:T(8,128)(2,1)}, u32[]{:S(2)}, u32[]{:S(2)}) collective-permute-start(bf16[2,2,256,128]{3,2,0,1:T(8,128)(2,1)S(1)} %bitcast.95), channel_id=1, source_target_pairs={{0,4},{2,6},{4,0},{6,2},{1,5},{3,7},{5,1},{7,3},{8,12},{10,14},{12... | collective-permute-start | bytes 786440 | tf_op jit(solution)/shard_map/ppermute | solution.py:16
  10.3 25.3 %collective-permute-start.3 = (bf16[2,2,256,128]{3,2,0,1:T(8,128)(2,1)S(1)}, bf16[2,2,256,128]{3,2,0,1:T(8,128)(2,1)}, u32[]{:S(2)}, u32[]{:S(2)}) collective-permute-start(bf16[2,2,256,128]{3,2,0,1:T(8,128)(2,1)S(1)} %bitcast.96), channel_id=1, source_target_pairs={{0,6},{2,4},{4,2},{6,0},{1,7},{3,5},{5,3},{7,1},{8,14},{10,12},{12... | collective-permute-start | bytes 786440 | tf_op jit(solution)/shard_map/ppermute | solution.py:16
  12.7 22.3 %collective-permute-start = (bf16[2,4,8,128]{3,2,1,0:T(8,128)(2,1)S(1)}, bf16[2,4,8,128]{3,2,1,0:T(8,128)(2,1)S(1)}, u32[]{:S(2)}, u32[]{:S(2)}) collective-permute-start(bf16[2,4,8,128]{3,2,1,0:T(8,128)(2,1)S(1)} %dynamic-slice_bitcast_fusion), channel_id=1, source_target_pairs={{0,1},{1,0},{2,3},{3,2},{4,5},{5,4},{6,7},{7,6},{8,9},{9,8},{10,11... | collective-permute-start | bytes 49160 | tf_op jit(solution)/shard_map/ppermute | solution.py:16
  17.0 16.9 %copy-start.5 = (s32[4]{0:T(128)S(1)}, s32[4]{0:T(128)}, u32[]{:S(2)}) copy-start(s32[4]{0:T(128)} %param.7) | copy-start | bytes 52
  17.0 17.1 %copy-start.3 = (bf16[2,2,4,2,1,128]{5,3,4,2,1,0:T(2,128)(2,1)S(1)}, bf16[2,2,4,2,1,128]{5,3,4,2,1,0:T(2,128)(2,1)}, u32[]{:S(2)}) copy-start(bf16[2,2,4,2,1,128]{5,3,4,2,1,0:T(2,128)(2,1)} %param.11) | copy-start | bytes 24580
  17.0 46.7 %all-to-all-start = ((bf16[64,2,4,8,128]{4,3,2,1,0:T(8,128)(2,1)}), bf16[64,2,4,8,128]{4,3,2,1,0:T(8,128)(2,1)S(1)}, u32[]{:S(2)}, u32[]{:S(2)}) async-start(bf16[64,2,4,8,128]{4,3,2,1,0:T(8,128)(2,1)} %shard_map.77), calls=%async_computation | async-start | bytes 2097152 | tf_op jit(solution)/shard_map/all_to_all | solution.py:124
  65.6 43.4 %all-to-all-start.1 = ((bf16[256,2,8,128]{3,2,1,0:T(8,128)(2,1)}), bf16[256,2,8,128]{3,2,1,0:T(8,128)(2,1)S(1)}, u32[]{:S(2)}, u32[]{:S(2)}) async-start(bf16[256,2,8,128]{3,2,1,0:T(8,128)(2,1)} %bitcast.38), calls=%async_computation.1 | async-start | bytes 2097152 | tf_op jit(solution)/shard_map/all_to_all | solution.py:214
  79.7 3.2 %collective-permute-start.4 = (f32[2,1,4,8,130]{4,3,2,1,0:T(8,128)S(1)}, f32[2,1,4,8,130]{4,3,2,1,0:T(8,128)S(1)}, u32[]{:S(2)}, u32[]{:S(2)}) collective-permute-start(f32[2,1,4,8,130]{4,3,2,1,0:T(8,128)S(1)} %copy.172), channel_id=1, source_target_pairs={{0,1},{1,0},{2,3},{3,2},{4,5},{5,4},{6,7},{7,6},{8,9},{9,8},{10,11... | collective-permute-start | bytes 99848 | tf_op jit(solution)/shard_map/ppermute | solution.py:16

commit v3 on v1

--- a/solution.py
+++ b/solution.py
@@ -7,6 +7,7 @@
 from jax.experimental.pallas import tpu as pltpu
 from jax.sharding import PartitionSpec as P
 
+
 MASKED = -1e30
 
 
@@ -32,28 +33,99 @@
     return (page_peak, weight_sum, page_output)
 
 
-def by_destination(keys, landed):
-    batches, slots, heads, rows, width = landed.shape
-
-    def body(keys_ref, landed_ref, out_ref):
-        def step(dest, carry):
-            for slot in range(slots):
-                source = dest ^ keys_ref[slot]
-                for head in range(heads):
-                    out_ref[dest, head, slot] = landed_ref[source, slot, head]
-            return carry
-
-        lax.fori_loop(0, batches, step, 0, unroll=4)
-
+def by_destination(key, landed):
+    batches, heads, rows, width = landed.shape
+
+    def body(key_ref, landed_ref, out_ref, ready, sent):
+        def outward(head):
+            return pltpu.make_async_copy(ready.at[head], out_ref.at[head], sent.at[head])
+
+        for head in range(heads):
+
+            def step(dest, carry):
+                ready[head, dest] = landed_ref[dest ^ key_ref[0], head]
+                return carry
+
+            lax.fori_loop(0, batches, step, 0, unroll=16)
+            outward(head).start()
+        for head in range(heads):
+            outward(head).wait()
+
+    shape = (heads, batches, rows, width)
     return pl.pallas_call(
         body,
-        out_shape=jax.ShapeDtypeStruct((batches, heads, slots, rows, width), landed.dtype),
+        out_shape=jax.ShapeDtypeStruct(shape, landed.dtype),
         in_specs=[
             pl.BlockSpec(memory_space=pltpu.SMEM),
             pl.BlockSpec(memory_space=pltpu.VMEM),
         ],
-        out_specs=pl.BlockSpec(memory_space=pltpu.VMEM),
-    )(keys, landed)
+        out_specs=pl.BlockSpec(memory_space=pltpu.HBM),
+        scratch_shapes=[pltpu.VMEM(shape, landed.dtype), pltpu.SemaphoreType.DMA((heads,))],
+        compiler_params=pltpu.CompilerParams(vmem_limit_bytes=4 * 2**20),
+    )(key, landed)
+
+
+def pieces_to_spread(raw, page_table, rows):
+    slots, kinds, heads, page_len, width = raw.shape
+    blocks = page_len // rows
+    req_count, max_pages = page_table.shape
+    chunks = [(slot, kind) for slot in range(slots) for kind in range(kinds)]
+
+    def body(table_ref, raw_ref, out_ref, table, here, ready, told, came, sent):
+        def inward(slot, kind):
+            return pltpu.make_async_copy(
+                raw_ref.at[slot, kind], here.at[slot, kind], came.at[slot, kind]
+            )
+
+        def outward(slot, kind):
+            return pltpu.make_async_copy(
+                ready.at[slot, kind], out_ref.at[slot, kind], sent.at[slot, kind]
+            )
+
+        lookup = pltpu.make_async_copy(table_ref, table, told)
+        lookup.start()
+        for chunk in chunks:
+            inward(*chunk).start()
+        first_slot = lax.axis_index("tensor") * slots
+        lookup.wait()
+        used = []
+        for slot in range(slots):
+            found = jnp.int32(0)
+            for row in range(req_count):
+                for column in range(max_pages):
+                    hit = table[row, column] == first_slot + slot
+                    found = jnp.where(hit, jnp.int32(1), found)
+            used.append(found > 0)
+        empty = jnp.zeros((rows, width), raw.dtype)
+        for slot, kind in chunks:
+            inward(slot, kind).wait()
+            for head in range(heads):
+                for block in range(blocks):
+                    piece = here[slot, kind, head, pl.ds(block * rows, rows)]
+                    ready[slot, kind, block, head] = jnp.where(used[slot], piece, empty)
+            outward(slot, kind).start()
+        for chunk in chunks:
+            outward(*chunk).wait()
+
+    shape = (slots, kinds, blocks, heads, rows, width)
+    return pl.pallas_call(
+        body,
+        out_shape=jax.ShapeDtypeStruct(shape, raw.dtype),
+        in_specs=[
+            pl.BlockSpec(memory_space=pltpu.HBM),
+            pl.BlockSpec(memory_space=pltpu.HBM),
+        ],
+        out_specs=pl.BlockSpec(memory_space=pltpu.HBM),
+        scratch_shapes=[
+            pltpu.SMEM(page_table.shape, page_table.dtype),
+            pltpu.VMEM(raw.shape, raw.dtype),
+            pltpu.VMEM(shape, raw.dtype),
+            pltpu.SemaphoreType.DMA,
+            pltpu.SemaphoreType.DMA((slots, kinds)),
+            pltpu.SemaphoreType.DMA((slots, kinds)),
+        ],
+        compiler_params=pltpu.CompilerParams(vmem_limit_bytes=63 * 2**20),
+    )(page_table, raw)
 
 
 def on_device(prefill_cache, lengths, page_table, holder, queries, new_kv):
@@ -63,33 +135,20 @@
     section_at = lax.axis_index("section")
     raw = prefill_cache[0]
     own_slots, kinds, heads, page_len, head_dim = raw.shape
-    blocks = batch_count // kinds
-    block_rows = page_len // blocks
+    piece_rows = own_slots * kinds * page_len // batch_count
     owned_rows, layers, step_count = (queries.shape[0], queries.shape[1], queries.shape[2])
     group_size = queries.shape[3]
     req_count, max_pages = page_table.shape
 
-    slot_ids = jnp.arange(positions, dtype=jnp.int32)
-    page_hits = (page_table[:, :, None] == slot_ids).astype(jnp.int32)
-    in_use = jnp.sum(page_hits, axis=(0, 1)) > 0
-
-    own_use = lax.dynamic_slice(in_use, (tensor_at * own_slots,), (own_slots,))
-    own_keys = lax.dynamic_slice(holder[0], (tensor_at * own_slots,), (own_slots,))
-    kept = jnp.where(own_use[:, None, None, None, None], raw, jnp.zeros((), raw.dtype))
-    pieces = jnp.transpose(
-        kept.reshape(own_slots, kinds, heads, blocks, block_rows, head_dim), (1, 3, 0, 2, 4, 5)
-    ).reshape(batch_count, own_slots, heads, block_rows, head_dim)
+    spread_at = lax.axis_index("batch") // (batch_count // own_slots)
+    relayed_key = lax.dynamic_slice(holder, (0, tensor_at * own_slots + spread_at), (1, 1))
+    pieces = pieces_to_spread(raw, page_table, piece_rows).reshape(
+        batch_count, heads, piece_rows, head_dim
+    )
     landed = lax.all_to_all(pieces, "batch", split_axis=0, concat_axis=0, tiled=True)
-
-    outgoing = by_destination(own_keys, landed).reshape(
-        batch_count * tensor_size, own_slots, block_rows, head_dim
-    )
-    arrived = lax.all_to_all(
-        outgoing, ("batch", "tensor"), split_axis=0, concat_axis=0, tiled=True
-    )
-    decode_pool = jnp.transpose(
-        arrived.reshape(batch_count, positions, block_rows, head_dim), (1, 0, 2, 3)
-    ).reshape(1, positions, kinds, 1, page_len, head_dim)
+    outgoing = by_destination(relayed_key.reshape(1), landed).reshape(
+        tensor_size * batch_count, piece_rows, head_dim
+    )
 
     def head_of(index):
         return lax.dynamic_index_in_dim(raw, index, 2, keepdims=False)
@@ -175,6 +234,9 @@
         .reshape(owned_rows, layers, step_count, group_size, head_dim)
         .astype(jnp.bfloat16)
     )
+
+    arrived = lax.all_to_all(outgoing, ("tensor", "batch"), split_axis=0, concat_axis=0, tiled=True)
+    decode_pool = arrived.reshape(1, positions, kinds, 1, page_len, head_dim)
     return (attended, decode_pool)
 
 
@@ -187,6 +249,7 @@
         P(("batch", "section"), None, None, "tensor", None),
         P(("batch", "section"), None, None, None, "tensor", None),
     )
+
     return jax.shard_map(
         on_device,
         mesh=mesh,

time: 112 us -> 111 us (level)
  the two profiles are of different devices: /device:TPU:8 before, /device:TPU:16 now
where the time goes in v3:
time: 111 us
  waiting for transfers between devices  48.6 us (44%)
  starting transfers between devices  43.1 us (39%)
  local copies, waits for them, and re-layouts  7.62 us (7%)
  other arithmetic  4.92 us (4%)
  Pallas kernels  3.78 us (3%)
  matrix products  1.63 us (1%)
    all_to_all x1, waiting for transfers between devices, on_device(): lax.all_to_all(pieces, 'batch', split_axis=0, concat_axis=0, tiled=True)  24.8 us
    all_to_all x1, waiting for transfers between devices, on_device(): lax.all_to_all(outgoing, ('tensor', 'batch'), split_axis=0, concat_axis=0...  23.1 us
    all_to_all x1, starting transfers between devices, on_device(): lax.all_to_all(pieces, 'batch', split_axis=0, concat_axis=0, tiled=True)  16.6 us
    ppermute x5, starting transfers between devices, partner_swap(): return lax.ppermute(value, axis, pairs)  14.3 us
    all_to_all x1, starting transfers between devices, on_device(): lax.all_to_all(outgoing, ('tensor', 'batch'), split_axis=0, concat_axis=0...  12.2 us
  transfers between devices with their start and end apart: 7, of which 3 were waited for; matrix products, arithmetic and copies ran while one was open for 11% of the time, Pallas kernels for 2%

profile of v3, /device:TPU:16, one launch (start us, length us, event | category | flops | bytes accessed | tf_op | source)
XLA Modules:
  0.0 110.8 jit_solution(7886059696622165380)
XLA Ops:
  0.6 0.0 copy-start
  0.7 1.3 %constant_dynamic-slice_fusion.5 = (bf16[1,2,2,1,256,128]{5,4,3,2,1,0:T(8,128)(2,1)S(1)}, bf16[1,2,2,1,256,128]{5,4,3,2,1,0:T(8,128)(2,1)S(1)}, bf16[1,2,2,1,256...) fusion(bf16[1,2,2,4,256,128]{5,4,3,2,1,0:T(8,128)(2,1)} %param.6, s32[]{:T(128)S(6)} %select_n.136, ...), kind=kLoop, calls=%fused_computation.72 | loop fusion | bytes 2097168 | tf_op jit(solution)/shard_map/jit(dynamic_index_in_dim)/dynamic_slice | solution.py:154
  2.0 0.0 copy-start.2
  2.0 3.4 %collective-permute-start.1 = (bf16[2,2,256,128]{3,2,0,1:T(8,128)(2,1)S(1)}, bf16[2,2,256,128]{3,2,0,1:T(8,128)(2,1)}, u32[]{:S(2)}, u32[]{:S(2)}) collective-permute-start(bf16[2,2,256,128]{3,2,0,1:T(8,128)(2,1)S(1)} %bitcast.91), channel_id=1, source_target_pairs={{0,2},{2,0},{4,6},{6,4},{1,3},{3,1},{5,7},{7,5},{8,10},{10,8},{12,... | collective-permute-start | bytes 786440 | tf_op jit(solution)/shard_map/ppermute | solution.py:16
  5.4 4.6 %collective-permute-start.2 = (bf16[2,2,256,128]{3,2,0,1:T(8,128)(2,1)S(1)}, bf16[2,2,256,128]{3,2,0,1:T(8,128)(2,1)}, u32[]{:S(2)}, u32[]{:S(2)}) collective-permute-start(bf16[2,2,256,128]{3,2,0,1:T(8,128)(2,1)S(1)} %bitcast.92), channel_id=1, source_target_pairs={{0,4},{2,6},{4,0},{6,2},{1,5},{3,7},{5,1},{7,3},{8,12},{10,14},{12... | collective-permute-start | bytes 786440 | tf_op jit(solution)/shard_map/ppermute | solution.py:16
  10.1 0.7 copy.186
  10.8 2.4 %collective-permute-start.3 = (bf16[2,2,256,128]{3,2,0,1:T(8,128)(2,1)}, bf16[2,2,256,128]{3,2,0,1:T(8,128)(2,1)}, u32[]{:S(2)}, u32[]{:S(2)}) collective-permute-start(bf16[2,2,256,128]{3,2,0,1:T(8,128)(2,1)} %bitcast.81), channel_id=1, source_target_pairs={{0,6},{2,4},{4,2},{6,0},{1,7},{3,5},{5,3},{7,1},{8,14},{10,12},{12... | collective-permute-start | bytes 786440 | tf_op jit(solution)/shard_map/ppermute | solution.py:16
  13.2 1.9 %collective-permute-start = (bf16[2,4,8,128]{3,2,1,0:T(8,128)(2,1)S(1)}, bf16[2,4,8,128]{3,2,1,0:T(8,128)(2,1)}, u32[]{:S(2)}, u32[]{:S(2)}) collective-permute-start(bf16[2,4,8,128]{3,2,1,0:T(8,128)(2,1)S(1)} %dynamic-slice_bitcast_fusion), channel_id=1, source_target_pairs={{0,1},{1,0},{2,3},{3,2},{4,5},{5,4},{6,7},{7,6},{8,9},{9,8},{10,11... | collective-permute-start | bytes 49160 | tf_op jit(solution)/shard_map/ppermute | solution.py:16
  15.2 2.0 %shard_map.77 = bf16[2,2,16,4,16,128]{5,4,3,2,1,0:T(8,128)(2,1)} custom-call(s32[4,5]{1,0:T(4,128)} %table_ref.1, bf16[2,2,4,256,128]{4,3,2,1,0:T(8,128)(2,1)} %bitcast.85), custom_call_target="tpu_custom_call" | custom-call | tf_op jit(solution)/shard_map/pallas_call | solution.py:111
  17.2 0.0 copy-start.3
  17.2 0.0 copy-start.4
  17.2 0.0 copy-start.1
  17.3 16.6 %all-to-all-start = ((bf16[64,4,16,128]{3,2,1,0:T(8,128)(2,1)}), bf16[64,4,16,128]{3,2,1,0:T(8,128)(2,1)S(1)}, u32[]{:S(2)}, u32[]{:S(2)}) async-start(bf16[64,4,16,128]{3,2,1,0:T(8,128)(2,1)} %bitcast.86), calls=%async_computation | async-start | bytes 2097152 | tf_op jit(solution)/shard_map/all_to_all | solution.py:148
  33.9 0.1 copy.152
  34.0 0.1 pad_add_fusion
  34.1 0.1 fusion.22
  34.3 0.1 iota_compare_fusion
  34.4 0.3 select_reduce_fusion.2
  34.7 0.3 fusion.35
  35.0 0.5 constant_dynamic-slice_fusion
  35.5 0.0 collective-permute-done
  35.5 0.7 bitcast_select_fusion.1
  36.3 0.6 gather_fusion
  36.9 1.2 %maximum_bitcast_fusion = bf16[8,2,1,256,128]{4,3,0,2,1:T(8,128)(2,1)S(1)} fusion(bf16[2,2,256,128]{3,2,0,1:T(8,128)(2,1)} %collective-permute-done.3, bf16[2,2,256,128]{3,2,0,1:T(8,128)(2,1)} %collective-permute-done.2, bf16[2,2,256,128]{3,2,0,1:T(8,128)(2,1)} %collective-permute-done.1, bf16[2,2,256,128]{3,2,0,1:T(8,128)(2,1)S(1)} %bitcast.89), kind=kLoop, calls=%fused_computation.10 | loop fusion | flops 1572864 | bytes 2097152 | tf_op jit(solution)/shard_map/broadcast_in_dim | solution.py:159
  38.1 0.4 select_reduce_fusion
  38.5 0.1 copy.157
  38.6 0.3 fusion.5
  38.9 24.8 %all-to-all-done.landed_ref = bf16[64,4,16,128]{3,2,1,0:T(8,128)(2,1)S(1)} async-done(((bf16[64,4,16,128]{3,2,1,0:T(8,128)(2,1)}), bf16[64,4,16,128]{3,2,1,0:T(8,128)(2,1)S(1)}, u32[]{:S(2)}, u32[]{:S(2)}) %all-to-all-start) | async-done | bytes 1048608 | tf_op jit(solution)/shard_map/all_to_all | solution.py:148
  63.7 1.7 %shard_map.78 = bf16[4,64,16,128]{3,2,1,0:T(8,128)(2,1)} custom-call(s32[1]{0:T(128)} %bitcast.37.key_ref, bf16[64,4,16,128]{3,2,1,0:T(8,128)(2,1)S(1)} %all-to-all-done.landed_ref), custom_call_target="tpu_custom_call" | custom-call | tf_op jit(solution)/shard_map/pallas_call | solution.py:55
  65.4 12.2 %all-to-all-start.1 = ((bf16[256,16,128]{2,1,0:T(8,128)(2,1)}), bf16[256,16,128]{2,1,0:T(8,128)(2,1)S(1)}, u32[]{:S(2)}, u32[]{:S(2)}) async-start(bf16[256,16,128]{2,1,0:T(8,128)(2,1)} %bitcast.40), calls=%async_computation.1 | async-start | bytes 2097152 | tf_op jit(solution)/shard_map/all_to_all | solution.py:238
  77.7 0.1 select_reduce_fusion.1
  77.8 0.1 copy.159
  77.9 0.4 fusion.7
  78.3 0.4 copy.161
  78.8 0.2 convert_reduce_fusion
  79.0 0.1 multiply_reduce_fusion
  79.1 0.3 pad_maximum_fusion
  79.4 0.3 copy.165
  79.7 1.9 %collective-permute-start.4 = (f32[2,1,4,8,130]{4,3,2,1,0:T(8,128)S(1)}, f32[2,1,4,8,130]{4,3,2,1,0:T(8,128)S(1)}, u32[]{:S(2)}, u32[]{:S(2)}) collective-permute-start(f32[2,1,4,8,130]{4,3,2,1,0:T(8,128)S(1)} %copy.165), channel_id=1, source_target_pairs={{0,1},{1,0},{2,3},{3,2},{4,5},{5,4},{6,7},{7,6},{8,9},{9,8},{10,11... | collective-permute-start | bytes 99848 | tf_op jit(solution)/shard_map/ppermute | solution.py:16
  81.7 0.1 convert_reduce_fusion.1
  81.8 0.4 copy.171
  82.2 0.7 collective-permute-done.4
  82.9 1.1 %copy.166 = f32[2,1,4,8,130]{3,2,4,0,1:T(4,128)} copy(f32[2,1,4,8,130]{4,3,2,1,0:T(8,128)S(1)} %collective-permute-done.4) | data formatting | bytes 66560 | tf_op jit(solution)/shard_map/ppermute | solution.py:16
  84.0 1.3 %select_bitcast_fusion.1 = (f32[2,1,1,4,8,130]{4,3,5,2,1,0:T(4,128)S(1)}, f32[2,1,1,4,8,130]{4,3,5,2,1,0:T(4,128)S(1)}) fusion(f32[2,1,4,8,130]{3,2,4,0,1:T(4,128)} %copy.166, f32[4,1,4,8,130]{3,2,4,0,1:T(4,128)S(1)} %pad_maximum_fusion, s32[]{:T(128)S(6)} %select_n.145, pred[]{:T(512)S(6)} %eq.33), kind=kLoop, calls=%fused_computation.13 | loop fusion | flops 16640 | bytes 133125 | tf_op jit(solution)/shard_map/stack | solution.py:206
  85.4 0.5 fusion.6
  85.9 0.8 copy.173
  86.7 23.1 %all-to-all-done.1 = bf16[256,16,128]{2,1,0:T(8,128)(2,1)S(1)} async-done(((bf16[256,16,128]{2,1,0:T(8,128)(2,1)}), bf16[256,16,128]{2,1,0:T(8,128)(2,1)S(1)}, u32[]{:S(2)}, u32[]{:S(2)}) %all-to-all-start.1) | async-done | bytes 1048608 | tf_op jit(solution)/shard_map/all_to_all | solution.py:238
  109.8 1.0 copy.191
  (31 shorter events, 0.3 us)
Async XLA Ops:
  0.6 34.4 %copy-start = (s32[64,8]{0,1:T(8,128)S(1)}, s32[64,8]{0,1:T(8,128)}, u32[]{:S(2)}) copy-start(s32[64,8]{0,1:T(8,128)} %param.9) | copy-start | bytes 6148
  2.0 11.2 %copy-start.2 = (bf16[2,2,4,8,128]{4,3,2,1,0:T(8,128)(2,1)S(1)}, bf16[2,2,4,8,128]{4,3,2,1,0:T(8,128)(2,1)}, u32[]{:S(2)}) copy-start(bf16[2,2,4,8,128]{4,3,2,1,0:T(8,128)(2,1)} %param.10) | copy-start | bytes 98308
  2.0 34.8 %collective-permute-start.1 = (bf16[2,2,256,128]{3,2,0,1:T(8,128)(2,1)S(1)}, bf16[2,2,256,128]{3,2,0,1:T(8,128)(2,1)}, u32[]{:S(2)}, u32[]{:S(2)}) collective-permute-start(bf16[2,2,256,128]{3,2,0,1:T(8,128)(2,1)S(1)} %bitcast.91), channel_id=1, source_target_pairs={{0,2},{2,0},{4,6},{6,4},{1,3},{3,1},{5,7},{7,5},{8,10},{10,8},{12,... | collective-permute-start | bytes 786440 | tf_op jit(solution)/shard_map/ppermute | solution.py:16
  5.4 31.4 %collective-permute-start.2 = (bf16[2,2,256,128]{3,2,0,1:T(8,128)(2,1)S(1)}, bf16[2,2,256,128]{3,2,0,1:T(8,128)(2,1)}, u32[]{:S(2)}, u32[]{:S(2)}) collective-permute-start(bf16[2,2,256,128]{3,2,0,1:T(8,128)(2,1)S(1)} %bitcast.92), channel_id=1, source_target_pairs={{0,4},{2,6},{4,0},{6,2},{1,5},{3,7},{5,1},{7,3},{8,12},{10,14},{12... | collective-permute-start | bytes 786440 | tf_op jit(solution)/shard_map/ppermute | solution.py:16
  10.8 26.0 %collective-permute-start.3 = (bf16[2,2,256,128]{3,2,0,1:T(8,128)(2,1)}, bf16[2,2,256,128]{3,2,0,1:T(8,128)(2,1)}, u32[]{:S(2)}, u32[]{:S(2)}) collective-permute-start(bf16[2,2,256,128]{3,2,0,1:T(8,128)(2,1)} %bitcast.81), channel_id=1, source_target_pairs={{0,6},{2,4},{4,2},{6,0},{1,7},{3,5},{5,3},{7,1},{8,14},{10,12},{12... | collective-permute-start | bytes 786440 | tf_op jit(solution)/shard_map/ppermute | solution.py:16
  13.2 22.3 %collective-permute-start = (bf16[2,4,8,128]{3,2,1,0:T(8,128)(2,1)S(1)}, bf16[2,4,8,128]{3,2,1,0:T(8,128)(2,1)}, u32[]{:S(2)}, u32[]{:S(2)}) collective-permute-start(bf16[2,4,8,128]{3,2,1,0:T(8,128)(2,1)S(1)} %dynamic-slice_bitcast_fusion), channel_id=1, source_target_pairs={{0,1},{1,0},{2,3},{3,2},{4,5},{5,4},{6,7},{7,6},{8,9},{9,8},{10,11... | collective-permute-start | bytes 49160 | tf_op jit(solution)/shard_map/ppermute | solution.py:16
  17.2 16.7 %copy-start.3 = (s32[4,5]{1,0:T(4,128)S(1)}, s32[4,5]{1,0:T(4,128)}, u32[]{:S(2)}) copy-start(s32[4,5]{1,0:T(4,128)} %table_ref.1) | copy-start | bytes 244
  17.2 16.9 %copy-start.4 = (s32[4]{0:T(128)S(1)}, s32[4]{0:T(128)}, u32[]{:S(2)}) copy-start(s32[4]{0:T(128)} %param.7) | copy-start | bytes 52
  17.2 17.0 %copy-start.1 = (bf16[2,2,4,2,1,128]{5,3,4,2,1,0:T(2,128)(2,1)S(1)}, bf16[2,2,4,2,1,128]{5,3,4,2,1,0:T(2,128)(2,1)}, u32[]{:S(2)}) copy-start(bf16[2,2,4,2,1,128]{5,3,4,2,1,0:T(2,128)(2,1)} %param.11) | copy-start | bytes 24580
  17.3 46.4 %all-to-all-start = ((bf16[64,4,16,128]{3,2,1,0:T(8,128)(2,1)}), bf16[64,4,16,128]{3,2,1,0:T(8,128)(2,1)S(1)}, u32[]{:S(2)}, u32[]{:S(2)}) async-start(bf16[64,4,16,128]{3,2,1,0:T(8,128)(2,1)} %bitcast.86), calls=%async_computation | async-start | bytes 2097152 | tf_op jit(solution)/shard_map/all_to_all | solution.py:148
  65.4 44.4 %all-to-all-start.1 = ((bf16[256,16,128]{2,1,0:T(8,128)(2,1)}), bf16[256,16,128]{2,1,0:T(8,128)(2,1)S(1)}, u32[]{:S(2)}, u32[]{:S(2)}) async-start(bf16[256,16,128]{2,1,0:T(8,128)(2,1)} %bitcast.40), calls=%async_computation.1 | async-start | bytes 2097152 | tf_op jit(solution)/shard_map/all_to_all | solution.py:238
  79.7 3.2 %collective-permute-start.4 = (f32[2,1,4,8,130]{4,3,2,1,0:T(8,128)S(1)}, f32[2,1,4,8,130]{4,3,2,1,0:T(8,128)S(1)}, u32[]{:S(2)}, u32[]{:S(2)}) collective-permute-start(f32[2,1,4,8,130]{4,3,2,1,0:T(8,128)S(1)} %copy.165), channel_id=1, source_target_pairs={{0,1},{1,0},{2,3},{3,2},{4,5},{5,4},{6,7},{7,6},{8,9},{9,8},{10,11... | collective-permute-start | bytes 99848 | tf_op jit(solution)/shard_map/ppermute | solution.py:16

commit v4 on v3

--- a/solution.py
+++ b/solution.py
@@ -40,10 +40,11 @@
         def outward(head):
             return pltpu.make_async_copy(ready.at[head], out_ref.at[head], sent.at[head])
 
+        own_key = jnp.max(key_ref[...])
         for head in range(heads):
 
             def step(dest, carry):
-                ready[head, dest] = landed_ref[dest ^ key_ref[0], head]
+                ready[head, dest] = landed_ref[dest ^ own_key, head]
                 return carry
 
             lax.fori_loop(0, batches, step, 0, unroll=16)
@@ -56,7 +57,7 @@
         body,
         out_shape=jax.ShapeDtypeStruct(shape, landed.dtype),
         in_specs=[
-            pl.BlockSpec(memory_space=pltpu.SMEM),
+            pl.BlockSpec(memory_space=pltpu.VMEM),
             pl.BlockSpec(memory_space=pltpu.VMEM),
         ],
         out_specs=pl.BlockSpec(memory_space=pltpu.HBM),
@@ -146,7 +147,7 @@
         batch_count, heads, piece_rows, head_dim
     )
     landed = lax.all_to_all(pieces, "batch", split_axis=0, concat_axis=0, tiled=True)
-    outgoing = by_destination(relayed_key.reshape(1), landed).reshape(
+    outgoing = by_destination(jnp.broadcast_to(relayed_key, (8, 128)), landed).reshape(
         tensor_size * batch_count, piece_rows, head_dim
     )
 

time: 111 us -> 112 us (level)
  no operation moved by 1% of the time
where the time goes in v4:
time: 112 us; the launch traced here: 111 us
  waiting for transfers between devices  48.6 us (43%)
  starting transfers between devices  43.1 us (38%)
  local copies, waits for them, and re-layouts  8.27 us (7%)
  other arithmetic  4.92 us (4%)
  Pallas kernels  3.33 us (3%)
  matrix products  1.63 us (1%)
    all_to_all x1, waiting for transfers between devices, on_device(): lax.all_to_all(pieces, 'batch', split_axis=0, concat_axis=0, tiled=True)  24.8 us
    all_to_all x1, waiting for transfers between devices, on_device(): lax.all_to_all(outgoing, ('tensor', 'batch'), split_axis=0, concat_axis=0...  23.1 us
    all_to_all x1, starting transfers between devices, on_device(): lax.all_to_all(pieces, 'batch', split_axis=0, concat_axis=0, tiled=True)  16.6 us
    ppermute x5, starting transfers between devices, partner_swap(): return lax.ppermute(value, axis, pairs)  14.3 us
    all_to_all x1, starting transfers between devices, on_device(): lax.all_to_all(outgoing, ('tensor', 'batch'), split_axis=0, concat_axis=0...  12.2 us
  transfers between devices with their start and end apart: 7, of which 3 were waited for; matrix products, arithmetic and copies ran while one was open for 11% of the time, Pallas kernels for 2%

profile of v4, /device:TPU:16, one launch (start us, length us, event | category | flops | bytes accessed | tf_op | source)
XLA Modules:
  0.0 111.0 jit_solution(6218421893268320786)
XLA Ops:
  0.6 0.0 copy-start
  0.7 1.3 %constant_dynamic-slice_fusion.5 = (bf16[1,2,2,1,256,128]{5,4,3,2,1,0:T(8,128)(2,1)S(1)}, bf16[1,2,2,1,256,128]{5,4,3,2,1,0:T(8,128)(2,1)S(1)}, bf16[1,2,2,1,256...) fusion(bf16[1,2,2,4,256,128]{5,4,3,2,1,0:T(8,128)(2,1)} %param.6, s32[]{:T(128)S(6)} %select_n.136, ...), kind=kLoop, calls=%fused_computation.72 | loop fusion | bytes 2097168 | tf_op jit(solution)/shard_map/jit(dynamic_index_in_dim)/dynamic_slice | solution.py:155
  2.0 0.0 copy-start.2
  2.0 3.4 %collective-permute-start.1 = (bf16[2,2,256,128]{3,2,0,1:T(8,128)(2,1)S(1)}, bf16[2,2,256,128]{3,2,0,1:T(8,128)(2,1)}, u32[]{:S(2)}, u32[]{:S(2)}) collective-permute-start(bf16[2,2,256,128]{3,2,0,1:T(8,128)(2,1)S(1)} %bitcast.91), channel_id=1, source_target_pairs={{0,2},{2,0},{4,6},{6,4},{1,3},{3,1},{5,7},{7,5},{8,10},{10,8},{12,... | collective-permute-start | bytes 786440 | tf_op jit(solution)/shard_map/ppermute | solution.py:16
  5.4 4.6 %collective-permute-start.2 = (bf16[2,2,256,128]{3,2,0,1:T(8,128)(2,1)S(1)}, bf16[2,2,256,128]{3,2,0,1:T(8,128)(2,1)}, u32[]{:S(2)}, u32[]{:S(2)}) collective-permute-start(bf16[2,2,256,128]{3,2,0,1:T(8,128)(2,1)S(1)} %bitcast.92), channel_id=1, source_target_pairs={{0,4},{2,6},{4,0},{6,2},{1,5},{3,7},{5,1},{7,3},{8,12},{10,14},{12... | collective-permute-start | bytes 786440 | tf_op jit(solution)/shard_map/ppermute | solution.py:16
  10.1 0.7 copy.186
  10.8 2.4 %collective-permute-start.3 = (bf16[2,2,256,128]{3,2,0,1:T(8,128)(2,1)}, bf16[2,2,256,128]{3,2,0,1:T(8,128)(2,1)}, u32[]{:S(2)}, u32[]{:S(2)}) collective-permute-start(bf16[2,2,256,128]{3,2,0,1:T(8,128)(2,1)} %bitcast.81), channel_id=1, source_target_pairs={{0,6},{2,4},{4,2},{6,0},{1,7},{3,5},{5,3},{7,1},{8,14},{10,12},{12... | collective-permute-start | bytes 786440 | tf_op jit(solution)/shard_map/ppermute | solution.py:16
  13.2 1.9 %collective-permute-start = (bf16[2,4,8,128]{3,2,1,0:T(8,128)(2,1)S(1)}, bf16[2,4,8,128]{3,2,1,0:T(8,128)(2,1)}, u32[]{:S(2)}, u32[]{:S(2)}) collective-permute-start(bf16[2,4,8,128]{3,2,1,0:T(8,128)(2,1)S(1)} %dynamic-slice_bitcast_fusion), channel_id=1, source_target_pairs={{0,1},{1,0},{2,3},{3,2},{4,5},{5,4},{6,7},{7,6},{8,9},{9,8},{10,11... | collective-permute-start | bytes 49160 | tf_op jit(solution)/shard_map/ppermute | solution.py:16
  15.2 2.0 %shard_map.77 = bf16[2,2,16,4,16,128]{5,4,3,2,1,0:T(8,128)(2,1)} custom-call(s32[4,5]{1,0:T(4,128)} %table_ref.1, bf16[2,2,4,256,128]{4,3,2,1,0:T(8,128)(2,1)} %bitcast.85), custom_call_target="tpu_custom_call" | custom-call | tf_op jit(solution)/shard_map/pallas_call | solution.py:112
  17.2 0.0 copy-start.3
  17.2 0.0 copy-start.4
  17.2 0.0 copy-start.1
  17.3 16.6 %all-to-all-start = ((bf16[64,4,16,128]{3,2,1,0:T(8,128)(2,1)}), bf16[64,4,16,128]{3,2,1,0:T(8,128)(2,1)S(1)}, u32[]{:S(2)}, u32[]{:S(2)}) async-start(bf16[64,4,16,128]{3,2,1,0:T(8,128)(2,1)} %bitcast.86), calls=%async_computation | async-start | bytes 2097152 | tf_op jit(solution)/shard_map/all_to_all | solution.py:149
  33.9 0.1 copy.152
  34.0 0.1 pad_add_fusion
  34.1 0.1 fusion.22
  34.3 0.1 iota_compare_fusion
  34.4 0.3 select_reduce_fusion.2
  34.7 0.3 fusion.35
  35.0 0.5 constant_dynamic-slice_fusion
  35.5 0.7 bitcast_select_fusion.1
  36.3 0.6 gather_fusion
  36.9 1.2 %maximum_bitcast_fusion = bf16[8,2,1,256,128]{4,3,0,2,1:T(8,128)(2,1)S(1)} fusion(bf16[2,2,256,128]{3,2,0,1:T(8,128)(2,1)} %collective-permute-done.3, bf16[2,2,256,128]{3,2,0,1:T(8,128)(2,1)} %collective-permute-done.2, bf16[2,2,256,128]{3,2,0,1:T(8,128)(2,1)} %collective-permute-done.1, bf16[2,2,256,128]{3,2,0,1:T(8,128)(2,1)S(1)} %bitcast.89), kind=kLoop, calls=%fused_computation.10 | loop fusion | flops 1572864 | bytes 2097152 | tf_op jit(solution)/shard_map/broadcast_in_dim | solution.py:160
  38.1 0.4 select_reduce_fusion
  38.5 0.1 copy.157
  38.6 0.3 fusion.5
  38.9 24.8 %all-to-all-done.landed_ref = bf16[64,4,16,128]{3,2,1,0:T(8,128)(2,1)S(1)} async-done(((bf16[64,4,16,128]{3,2,1,0:T(8,128)(2,1)}), bf16[64,4,16,128]{3,2,1,0:T(8,128)(2,1)S(1)}, u32[]{:S(2)}, u32[]{:S(2)}) %all-to-all-start) | async-done | bytes 1048608 | tf_op jit(solution)/shard_map/all_to_all | solution.py:149
  63.7 0.6 broadcast_in_dim.136.key_ref
  64.3 1.3 %shard_map.78 = bf16[4,64,16,128]{3,2,1,0:T(8,128)(2,1)} custom-call(s32[8,128]{1,0:T(8,128)S(1)} %broadcast_in_dim.136.key_ref, bf16[64,4,16,128]{3,2,1,0:T(8,128)(2,1)S(1)} %all-to-all-done.landed_ref), custom_call_target="tpu_custom_call" | custom-call | tf_op jit(solution)/shard_map/pallas_call | solution.py:56
  65.6 12.2 %all-to-all-start.1 = ((bf16[256,16,128]{2,1,0:T(8,128)(2,1)}), bf16[256,16,128]{2,1,0:T(8,128)(2,1)S(1)}, u32[]{:S(2)}, u32[]{:S(2)}) async-start(bf16[256,16,128]{2,1,0:T(8,128)(2,1)} %bitcast.40), calls=%async_computation.1 | async-start | bytes 2097152 | tf_op jit(solution)/shard_map/all_to_all | solution.py:239
  77.9 0.1 select_reduce_fusion.1
  78.0 0.1 copy.159
  78.1 0.4 fusion.7
  78.5 0.4 copy.161
  78.9 0.2 convert_reduce_fusion
  79.2 0.1 multiply_reduce_fusion
  79.3 0.3 pad_maximum_fusion
  79.6 0.3 copy.165
  79.9 1.9 %collective-permute-start.4 = (f32[2,1,4,8,130]{4,3,2,1,0:T(8,128)S(1)}, f32[2,1,4,8,130]{4,3,2,1,0:T(8,128)S(1)}, u32[]{:S(2)}, u32[]{:S(2)}) collective-permute-start(f32[2,1,4,8,130]{4,3,2,1,0:T(8,128)S(1)} %copy.165), channel_id=1, source_target_pairs={{0,1},{1,0},{2,3},{3,2},{4,5},{5,4},{6,7},{7,6},{8,9},{9,8},{10,11... | collective-permute-start | bytes 99848 | tf_op jit(solution)/shard_map/ppermute | solution.py:16
  81.9 0.1 convert_reduce_fusion.1
  82.0 0.4 copy.171
  82.4 0.7 collective-permute-done.4
  83.1 1.1 %copy.166 = f32[2,1,4,8,130]{3,2,4,0,1:T(4,128)} copy(f32[2,1,4,8,130]{4,3,2,1,0:T(8,128)S(1)} %collective-permute-done.4) | data formatting | bytes 66560 | tf_op jit(solution)/shard_map/ppermute | solution.py:16
  84.2 1.3 %select_bitcast_fusion.1 = (f32[2,1,1,4,8,130]{4,3,5,2,1,0:T(4,128)S(1)}, f32[2,1,1,4,8,130]{4,3,5,2,1,0:T(4,128)S(1)}) fusion(f32[2,1,4,8,130]{3,2,4,0,1:T(4,128)} %copy.166, f32[4,1,4,8,130]{3,2,4,0,1:T(4,128)S(1)} %pad_maximum_fusion, s32[]{:T(128)S(6)} %select_n.145, pred[]{:T(512)S(6)} %eq.33), kind=kLoop, calls=%fused_computation.13 | loop fusion | flops 16640 | bytes 133125 | tf_op jit(solution)/shard_map/stack | solution.py:207
  85.6 0.5 fusion.6
  86.1 0.8 copy.173
  86.9 23.1 %all-to-all-done.1 = bf16[256,16,128]{2,1,0:T(8,128)(2,1)S(1)} async-done(((bf16[256,16,128]{2,1,0:T(8,128)(2,1)}), bf16[256,16,128]{2,1,0:T(8,128)(2,1)S(1)}, u32[]{:S(2)}, u32[]{:S(2)}) %all-to-all-start.1) | async-done | bytes 1048608 | tf_op jit(solution)/shard_map/all_to_all | solution.py:239
  110.0 1.0 copy.191
  (32 shorter events, 0.3 us)
Async XLA Ops:
  0.6 34.4 %copy-start = (s32[64,8]{0,1:T(8,128)S(1)}, s32[64,8]{0,1:T(8,128)}, u32[]{:S(2)}) copy-start(s32[64,8]{0,1:T(8,128)} %param.9) | copy-start | bytes 6148
  2.0 11.2 %copy-start.2 = (bf16[2,2,4,8,128]{4,3,2,1,0:T(8,128)(2,1)S(1)}, bf16[2,2,4,8,128]{4,3,2,1,0:T(8,128)(2,1)}, u32[]{:S(2)}) copy-start(bf16[2,2,4,8,128]{4,3,2,1,0:T(8,128)(2,1)} %param.10) | copy-start | bytes 98308
  2.0 34.8 %collective-permute-start.1 = (bf16[2,2,256,128]{3,2,0,1:T(8,128)(2,1)S(1)}, bf16[2,2,256,128]{3,2,0,1:T(8,128)(2,1)}, u32[]{:S(2)}, u32[]{:S(2)}) collective-permute-start(bf16[2,2,256,128]{3,2,0,1:T(8,128)(2,1)S(1)} %bitcast.91), channel_id=1, source_target_pairs={{0,2},{2,0},{4,6},{6,4},{1,3},{3,1},{5,7},{7,5},{8,10},{10,8},{12,... | collective-permute-start | bytes 786440 | tf_op jit(solution)/shard_map/ppermute | solution.py:16
  5.4 31.4 %collective-permute-start.2 = (bf16[2,2,256,128]{3,2,0,1:T(8,128)(2,1)S(1)}, bf16[2,2,256,128]{3,2,0,1:T(8,128)(2,1)}, u32[]{:S(2)}, u32[]{:S(2)}) collective-permute-start(bf16[2,2,256,128]{3,2,0,1:T(8,128)(2,1)S(1)} %bitcast.92), channel_id=1, source_target_pairs={{0,4},{2,6},{4,0},{6,2},{1,5},{3,7},{5,1},{7,3},{8,12},{10,14},{12... | collective-permute-start | bytes 786440 | tf_op jit(solution)/shard_map/ppermute | solution.py:16
  10.8 26.0 %collective-permute-start.3 = (bf16[2,2,256,128]{3,2,0,1:T(8,128)(2,1)}, bf16[2,2,256,128]{3,2,0,1:T(8,128)(2,1)}, u32[]{:S(2)}, u32[]{:S(2)}) collective-permute-start(bf16[2,2,256,128]{3,2,0,1:T(8,128)(2,1)} %bitcast.81), channel_id=1, source_target_pairs={{0,6},{2,4},{4,2},{6,0},{1,7},{3,5},{5,3},{7,1},{8,14},{10,12},{12... | collective-permute-start | bytes 786440 | tf_op jit(solution)/shard_map/ppermute | solution.py:16
  13.2 22.3 %collective-permute-start = (bf16[2,4,8,128]{3,2,1,0:T(8,128)(2,1)S(1)}, bf16[2,4,8,128]{3,2,1,0:T(8,128)(2,1)}, u32[]{:S(2)}, u32[]{:S(2)}) collective-permute-start(bf16[2,4,8,128]{3,2,1,0:T(8,128)(2,1)S(1)} %dynamic-slice_bitcast_fusion), channel_id=1, source_target_pairs={{0,1},{1,0},{2,3},{3,2},{4,5},{5,4},{6,7},{7,6},{8,9},{9,8},{10,11... | collective-permute-start | bytes 49160 | tf_op jit(solution)/shard_map/ppermute | solution.py:16
  17.2 16.7 %copy-start.3 = (s32[4,5]{1,0:T(4,128)S(1)}, s32[4,5]{1,0:T(4,128)}, u32[]{:S(2)}) copy-start(s32[4,5]{1,0:T(4,128)} %table_ref.1) | copy-start | bytes 244
  17.2 16.9 %copy-start.4 = (s32[4]{0:T(128)S(1)}, s32[4]{0:T(128)}, u32[]{:S(2)}) copy-start(s32[4]{0:T(128)} %param.7) | copy-start | bytes 52
  17.2 17.0 %copy-start.1 = (bf16[2,2,4,2,1,128]{5,3,4,2,1,0:T(2,128)(2,1)S(1)}, bf16[2,2,4,2,1,128]{5,3,4,2,1,0:T(2,128)(2,1)}, u32[]{:S(2)}) copy-start(bf16[2,2,4,2,1,128]{5,3,4,2,1,0:T(2,128)(2,1)} %param.11) | copy-start | bytes 24580
  17.3 46.4 %all-to-all-start = ((bf16[64,4,16,128]{3,2,1,0:T(8,128)(2,1)}), bf16[64,4,16,128]{3,2,1,0:T(8,128)(2,1)S(1)}, u32[]{:S(2)}, u32[]{:S(2)}) async-start(bf16[64,4,16,128]{3,2,1,0:T(8,128)(2,1)} %bitcast.86), calls=%async_computation | async-start | bytes 2097152 | tf_op jit(solution)/shard_map/all_to_all | solution.py:149
  65.6 44.4 %all-to-all-start.1 = ((bf16[256,16,128]{2,1,0:T(8,128)(2,1)}), bf16[256,16,128]{2,1,0:T(8,128)(2,1)S(1)}, u32[]{:S(2)}, u32[]{:S(2)}) async-start(bf16[256,16,128]{2,1,0:T(8,128)(2,1)} %bitcast.40), calls=%async_computation.1 | async-start | bytes 2097152 | tf_op jit(solution)/shard_map/all_to_all | solution.py:239
  79.9 3.2 %collective-permute-start.4 = (f32[2,1,4,8,130]{4,3,2,1,0:T(8,128)S(1)}, f32[2,1,4,8,130]{4,3,2,1,0:T(8,128)S(1)}, u32[]{:S(2)}, u32[]{:S(2)}) collective-permute-start(f32[2,1,4,8,130]{4,3,2,1,0:T(8,128)S(1)} %copy.165), channel_id=1, source_target_pairs={{0,1},{1,0},{2,3},{3,2},{4,5},{5,4},{6,7},{7,6},{8,9},{9,8},{10,11... | collective-permute-start | bytes 99848 | tf_op jit(solution)/shard_map/ppermute | solution.py:16
